TPU v7x, 32 devices: a whole 2x2x4 slice. The times are simulated.
32 devices in a mesh: member: 8 (over z, core), region: 4 (over y, x).
Axes of the slice: x: 2, y: 2, z: 4, core: 2. Of those that a mesh axis runs over, the one named last changes fastest.
Arguments:
- prior_states: bfloat16 [512, 65536], P('member', 'region'), may hold values from -6 to 6
- measured_values: bfloat16 [8192], P('region'), may hold values from -12 to 12
- measurement_precision: bfloat16 [8192], P('region'), may hold values from 0.5 to 4
- measured_subgrid_line: int32 [8192], P('region'), may hold values from 0 to 16383, as said below
- neighbour_measurement_lookup: int32 [4, 8, 1024], P('region'), may hold values from 0 to 6143, as said below
- active_entries_tally: int32 [4, 8], P('region', 'member'), may hold values from 512 to 1024, as said below
- distance_tier: int32 [4, 8, 1024], P('region', 'member'), may hold values from 0 to 8
- eastward_weight_share: int32 [4, 8, 2048], P('region', 'member'), may hold values from 0 to 8
Outputs:
- analysis: bfloat16 [512, 65536], P('member', 'region')
Inputs may be any that keep to these rules, and one draw needn't show every extreme that they name: `neighbour_measurement_lookup`: for coarse point (s, p) the live and dead slots name distinct observations, all in blocks p-1, p, p+1 (each block 256 observations of a sector, in order) of sectors s-1, s, s+1; blocks outside 0 to 7 are never named. `measured_subgrid_line`: observation o of a sector measures a row of its block: from ((o % 2048) // 256) * 2048 to that plus 2048 - 1. `active_entries_tally`: some coarse point has all 1024 slots live.
All inputs are finite; a program needn't handle non-finite values.
Results may differ from a plain program's by a relative error of at most 0.019.
Values may be sent and summed in bfloat16 or wider, within the bound.
No kernel may reach another device: no remote copies, remote signals or barrier semaphores. Data moves between devices by JAX's collectives and lax.ppermute only.
A program may use at most 64 MiB of HBM per device.

v0:
```python
import functools

import jax
import jax.numpy as jnp
from jax import lax
from jax.experimental import pallas as pl
from jax.experimental.pallas import tpu as pltpu
from jax.sharding import PartitionSpec as P


ITERS = 6

VMEM = pltpu.MemorySpace.VMEM
HBM = pltpu.MemorySpace.HBM


def nt_dot(a, b):
    return lax.dot_general(a, b, (((1,), (1,)), ((), ())), preferred_element_type=jnp.float32)


def partner(me, d, count):
    if count & (count - 1) == 0:
        return me ^ d
    return (me + d) % count


def source(me, d, count):
    if count & (count - 1) == 0:
        return me ^ d
    return (me + count - d) % count


def gather_kernel(line_ref, x_ref, out_ref):
    rows = x_ref.shape[1]
    width = line_ref.shape[1]
    line = line_ref[...] - pl.program_id(0) * rows
    hot = (lax.broadcasted_iota(jnp.int32, (rows, width), 0) == line).astype(jnp.bfloat16)
    out_ref[0] = jnp.dot(x_ref[...], hot, preferred_element_type=jnp.float32).astype(jnp.bfloat16)


def gather_obs(prior, line, bands):
    members, fine = prior.shape
    rows = fine // bands
    width = line.shape[0] // bands
    return pl.pallas_call(
        gather_kernel,
        grid=(bands,),
        in_specs=[
            pl.BlockSpec((1, width), lambda b: (0, b)),
            pl.BlockSpec((members, rows), lambda b: (0, b)),
        ],
        out_specs=pl.BlockSpec((1, members, width), lambda b: (b, 0, 0)),
        out_shape=jax.ShapeDtypeStruct((bands, members, width), jnp.bfloat16),
        name="gather_obs",
    )(line.reshape(1, -1), prior)


def candidate_kernel(bands, count_ref, lookup_ref, dist_ref, low_ref, own_ref, high_ref, w_ref, val_ref):
    me = lax.axis_index("member")
    slots = lookup_ref.shape[1]
    obs_tile = own_ref.shape[1]
    width = obs_tile // bands
    index = lookup_ref[pl.ds(me, 1), :]
    live = lax.broadcasted_iota(jnp.int32, (1, slots), 1) < count_ref[0, 0]
    denom = jnp.where(live, 2.0 + dist_ref[...].astype(jnp.float32), 0.0)
    denom = jnp.broadcast_to(denom, (8, slots)).astype(jnp.bfloat16)
    rows = lax.broadcasted_iota(jnp.int32, (width, slots), 0)
    for off in range(3):
        band = me + off - 1
        valid = jnp.logical_and(band >= 0, band < bands)
        start = pl.multiple_of(jnp.clip(band, 0, bands - 1) * width, width)
        for side, ref in enumerate((low_ref, own_ref, high_ref)):
            base = jnp.where(valid, side * obs_tile + band * width, -4 * obs_tile)
            hot = (rows == index - base).astype(jnp.bfloat16)
            total = nt_dot(denom, hot)[0:1]
            pair = ref[:, pl.ds(start, width)].astype(jnp.float32)
            named = total > 0.0
            weight = pair[1:2] * 2.0 / jnp.where(named, total, 1.0)
            j = off * 3 + side
            w_ref[j : j + 1, :] = jnp.where(named, weight, 0.0)
            val_ref[j : j + 1, :] = pair[0:1]


def candidates(count, lookup, dist, low, own, high, bands):
    width = own.shape[1] // bands
    shape = jax.ShapeDtypeStruct((9, width), jnp.float32)
    return pl.pallas_call(
        functools.partial(candidate_kernel, bands),
        in_specs=[pl.BlockSpec(memory_space=pltpu.MemorySpace.SMEM)] + [pl.BlockSpec(memory_space=VMEM)] * 5,
        out_specs=[pl.BlockSpec(memory_space=VMEM)] * 2,
        out_shape=[shape, shape],
        name="candidates",
    )(count, lookup, dist, low, own, high)


def transform_kernel(
    count, before_ref, mid_ref, after_ref, w_ref, val_ref, near_ref, far_ref, pert_ref, weighted_ref, wt_ref
):
    members = wt_ref.shape[0]
    width = w_ref.shape[1]
    gvec = jnp.zeros((members, 1), jnp.float32)
    for off, ref in enumerate((before_ref, mid_ref, after_ref)):
        for side in range(3):
            j = off * 3 + side
            values = ref[side].astype(jnp.float32)
            ybar = jnp.mean(values, axis=0, keepdims=True)
            pert = (values - ybar).astype(jnp.bfloat16)
            weighted = pert.astype(jnp.float32) * w_ref[j : j + 1, :]
            gvec = gvec + jnp.sum(weighted * (val_ref[j : j + 1, :] - ybar), axis=1, keepdims=True)
            pert_ref[:, j * width : (j + 1) * width] = pert
            weighted_ref[:, j * width : (j + 1) * width] = weighted.astype(jnp.bfloat16)
    gram = nt_dot(weighted_ref[...], pert_ref[...])
    row = lax.broadcasted_iota(jnp.int32, (members, members), 0)
    col = lax.broadcasted_iota(jnp.int32, (members, members), 1)
    eye = row == col
    amat = gram + jnp.where(eye, members - 1.0, 0.0)
    norm = jnp.sqrt(jnp.sum(jnp.sum(amat * amat, axis=1, keepdims=True), axis=0, keepdims=True))
    zmat = (amat / norm).astype(jnp.bfloat16)
    ident = jnp.where(eye, 1.5, 0.0)

    def mm(a, b):
        return jnp.dot(a, b, preferred_element_type=jnp.float32)

    tmat = (ident - 0.5 * zmat.astype(jnp.float32)).astype(jnp.bfloat16)
    ymat = tmat
    zmat = mm(tmat, zmat).astype(jnp.bfloat16)
    for step in range(1, ITERS):
        tmat = (ident - 0.5 * mm(zmat, ymat)).astype(jnp.bfloat16)
        ymat = mm(ymat, tmat).astype(jnp.bfloat16)
        if step < ITERS - 1:
            zmat = mm(tmat, zmat).astype(jnp.bfloat16)
    isq = ymat.astype(jnp.float32) / jnp.sqrt(norm)

    def as_row(column):
        return jnp.sum(jnp.where(eye, column, 0.0), axis=0, keepdims=True)

    once = jnp.sum(isq * as_row(gvec), axis=1, keepdims=True)
    wbar = jnp.sum(isq * as_row(once), axis=1, keepdims=True)
    wt_ref[...] = (jnp.sqrt(members - 1.0) * isq + as_row(wbar)).astype(jnp.bfloat16)
    me = lax.axis_index("member")
    each = members // count
    half = count // 2
    for d in range(count):
        rows = wt_ref[pl.ds(pl.multiple_of(partner(me, d, count) * each, each), each), :]
        if d < half:
            near_ref[d * each : (d + 1) * each, :] = rows
        else:
            far_ref[(d - half) * each : (d - half + 1) * each, :] = rows


def transform(before, mid, after, w, val, count):
    members = mid.shape[1]
    width = mid.shape[2]
    each = members // count
    half = count // 2
    return pl.pallas_call(
        functools.partial(transform_kernel, count),
        in_specs=[pl.BlockSpec(memory_space=VMEM)] * 5,
        out_specs=[pl.BlockSpec(memory_space=VMEM)] * 2,
        out_shape=[
            jax.ShapeDtypeStruct((half * each, members), jnp.bfloat16),
            jax.ShapeDtypeStruct(((count - half) * each, members), jnp.bfloat16),
        ],
        scratch_shapes=[
            pltpu.VMEM((members, 9 * width), jnp.bfloat16),
            pltpu.VMEM((members, 9 * width), jnp.bfloat16),
            pltpu.VMEM((members, members), jnp.bfloat16),
        ],
        name="transform",
    )(before, mid, after, w, val)


def analysis(wt_ref, we_ref, level_ref, xbar, xp, cols, outs):
    own = jnp.dot(wt_ref[...], xp, preferred_element_type=jnp.float32)
    east = jnp.dot(we_ref[...], xp, preferred_element_type=jnp.float32)
    share = level_ref[:, cols].astype(jnp.float32) / 8.0
    result = (xbar + (1.0 - share) * own + share * east).astype(jnp.bfloat16)
    each = outs[0].shape[0]
    for place, out in enumerate(outs):
        out[:, cols] = result[place * each : (place + 1) * each]


def far_kernel(count, wt_ref, we_ref, level_ref, *refs):
    ins, xbar_ref, xp_ref, outs = refs[:count], refs[count], refs[count + 1], refs[count + 2 : -2]
    x_ref, sem = refs[-2:]
    me = lax.axis_index("member")
    each, rows = ins[1].shape
    loads = []
    for d in range(count):
        to = x_ref.at[pl.ds(pl.multiple_of(source(me, d, count) * each, each), each), :]
        loads.append(pltpu.make_async_copy(ins[d], to, sem.at[d]))
        loads[-1].start()
    for load in loads:
        load.wait()
    step = min(rows, 512)
    for at in range(0, rows, step):
        cols = slice(at, at + step)
        values = x_ref[:, cols].astype(jnp.float32)
        xbar = jnp.mean(values, axis=0, keepdims=True)
        xp = (values - xbar).astype(jnp.bfloat16)
        xbar_ref[:, cols] = xbar
        xp_ref[:, cols] = xp
        analysis(wt_ref, we_ref, level_ref, xbar, xp, cols, outs)


def far_update(wt, we, level, blocks):
    count = len(blocks)
    each, rows = blocks[0].shape
    members = each * count
    part = wt.shape[0] // each
    return pl.pallas_call(
        functools.partial(far_kernel, count),
        in_specs=[pl.BlockSpec(memory_space=VMEM)] * 3 + [pl.BlockSpec(memory_space=HBM)] * count,
        out_specs=[pl.BlockSpec(memory_space=VMEM)] * (2 + part),
        out_shape=[
            jax.ShapeDtypeStruct((1, rows), jnp.float32),
            jax.ShapeDtypeStruct((members, rows), jnp.bfloat16),
        ]
        + [jax.ShapeDtypeStruct((each, rows), jnp.bfloat16)] * part,
        scratch_shapes=[pltpu.VMEM((members, rows), jnp.bfloat16), pltpu.SemaphoreType.DMA((count,))],
        name="far_update",
    )(wt, we, level, *blocks)


def near_kernel(wt_ref, we_ref, level_ref, xbar_ref, xp_ref, *outs):
    rows = xp_ref.shape[1]
    step = min(rows, 512)
    for at in range(0, rows, step):
        cols = slice(at, at + step)
        analysis(wt_ref, we_ref, level_ref, xbar_ref[:, cols], xp_ref[:, cols], cols, outs)


def near_update(wt, we, level, xbar, xp, each):
    rows = xp.shape[1]
    part = wt.shape[0] // each
    return pl.pallas_call(
        near_kernel,
        in_specs=[pl.BlockSpec(memory_space=VMEM)] * 5,
        out_specs=[pl.BlockSpec(memory_space=VMEM)] * part,
        out_shape=[jax.ShapeDtypeStruct((each, rows), jnp.bfloat16)] * part,
        name="near_update",
    )(wt, we, level, xbar, xp)


def assemble_kernel(count, *refs):
    ins, out_ref, sem = refs[:count], refs[count], refs[count + 1]
    me = lax.axis_index("member")
    rows = ins[0].shape[1]
    copies = []
    for d in range(count):
        to = out_ref.at[:, pl.ds(pl.multiple_of(source(me, d, count) * rows, rows), rows)]
        copies.append(pltpu.make_async_copy(ins[d], to, sem.at[d]))
        copies[-1].start()
    for copy in copies:
        copy.wait()


def assemble(blocks):
    count = len(blocks)
    each, rows = blocks[0].shape
    return pl.pallas_call(
        functools.partial(assemble_kernel, count),
        in_specs=[pl.BlockSpec(memory_space=VMEM)] * count,
        out_specs=pl.BlockSpec(memory_space=HBM),
        out_shape=jax.ShapeDtypeStruct((each, rows * count), jnp.bfloat16),
        scratch_shapes=[pltpu.SemaphoreType.DMA((count,))],
        name="assemble",
    )(*blocks)


def local(
    prior_states,
    measured_values,
    measurement_precision,
    measured_subgrid_line,
    neighbour_measurement_lookup,
    active_entries_tally,
    distance_tier,
    eastward_weight_share,
):
    bands = lax.axis_size("member")
    sectors = lax.axis_size("region")
    me = lax.axis_index("member")
    each, fine = prior_states.shape
    rows = fine // bands
    east = [(i, (i + 1) % sectors) for i in range(sectors)]
    west = [(target, origin) for origin, target in east]
    north = [(i, i + 1) for i in range(bands - 1)]
    south = [(i + 1, i) for i in range(bands - 1)]

    half = bands // 2

    def block_for(d):
        return lax.dynamic_slice_in_dim(prior_states, partner(me, d, bands) * rows, rows, axis=1)

    def trade(value, d):
        return lax.ppermute(value, "member", [(i, partner(i, d, bands)) for i in range(bands)])

    states = [block_for(0)] + [trade(block_for(d), d) for d in range(1, bands)]
    paired = jnp.stack((measured_values, measurement_precision))
    pair_low = lax.ppermute(paired, "region", east)
    pair_high = lax.ppermute(paired, "region", west)

    proj = gather_obs(prior_states, measured_subgrid_line, bands)
    own = lax.all_to_all(proj, "member", split_axis=0, concat_axis=0, tiled=True)
    own = own.reshape(each * bands, -1)
    low = lax.ppermute(own, "region", east)
    high = lax.ppermute(own, "region", west)
    mid = jnp.stack((low, own, high))
    before = lax.ppermute(mid, "member", north)
    after = lax.ppermute(mid, "member", south)
    w, val = candidates(
        active_entries_tally, neighbour_measurement_lookup[0], distance_tier[0], pair_low, paired, pair_high, bands
    )
    wt_near, wt_far = transform(before, mid, after, w, val, bands)
    we_far = lax.ppermute(wt_far, "region", west)
    we_near = lax.ppermute(wt_near, "region", west)
    level = eastward_weight_share[0]
    xbar, xp, *far = far_update(wt_far, we_far, level, states)
    back_far = [trade(far[d - half], d) for d in range(half, bands)]
    near = near_update(wt_near, we_near, level, xbar, xp, each)
    back_near = [near[0]] + [trade(near[d], d) for d in range(1, half)]
    return assemble(back_near + back_far)


def solution(mesh):
    in_specs = (
        P("member", "region"),
        P("region"),
        P("region"),
        P("region"),
        P("region", None, None),
        P("region", "member"),
        P("region", "member", None),
        P("region", "member", None),
    )
    out_specs = P("member", "region")
    return jax.shard_map(local, mesh=mesh, in_specs=in_specs, out_specs=out_specs, check_vma=False)
```

profile of v0, /device:TPU:9, one launch (start us, length us, event | category | flops | bytes accessed | tf_op | source)
XLA Modules:
  0.0 158.6 jit_solution(495514483401094575)
XLA Ops:
  0.0 6.6 %gather_obs.1 = bf16[8,64,256]{2,1,0:T(8,128)(2,1)} custom-call(s32[1,2048]{1,0:T(1,128)} %bitcast.16, bf16[64,16384]{1,0:T(8,128)(2,1)} %x_ref.1), custom_call_target="tpu_custom_call" | custom-call | tf_op jit(solution)/shard_map/gather_obs/pallas_call | solution.py:45
  6.6 12.7 %all_to_all.5 = bf16[8,64,256]{2,1,0:T(8,128)(2,1)S(1)} all-to-all(bf16[8,64,256]{2,1,0:T(8,128)(2,1)} %gather_obs.1), channel_id=1, replica_groups=mesh['member'=8,'region'=4] {'member'}, dimensions={0} | all-to-all | bytes 524288 | tf_op jit(solution)/shard_map/all_to_all | solution.py:305
  19.3 1.2 collective-permute-start
  20.5 1.2 collective-permute-start.1
  21.6 5.4 %collective-permute-done = bf16[512,256]{1,0:T(8,128)(2,1)S(1)} collective-permute-done((bf16[512,256]{1,0:T(8,128)(2,1)S(1)}, bf16[512,256]{1,0:T(8,128)(2,1)S(1)}, u32[]{:S(2)}, u32[]{:S(2)}) %collective-permute-start) | collective-permute-done | bytes 262176 | tf_op jit(solution)/shard_map/ppermute | solution.py:307
  27.0 5.7 %collective-permute-done.1 = bf16[512,256]{1,0:T(8,128)(2,1)S(1)} collective-permute-done((bf16[512,256]{1,0:T(8,128)(2,1)S(1)}, bf16[512,256]{1,0:T(8,128)(2,1)S(1)}, u32[]{:S(2)}, u32[]{:S(2)}) %collective-permute-start.1) | collective-permute-done | bytes 262176 | tf_op jit(solution)/shard_map/ppermute | solution.py:308
  32.7 0.1 pad_maximum_fusion.mid_ref
  32.8 0.0 copy-start.1
  32.8 3.4 %collective-permute-start.2 = (bf16[3,512,256]{2,1,0:T(8,128)(2,1)S(1)}, bf16[3,512,256]{2,1,0:T(8,128)(2,1)}, u32[]{:S(2)}, u32[]{:S(2)}) collective-permute-start(bf16[3,512,256]{2,1,0:T(8,128)(2,1)S(1)} %pad_maximum_fusion.mid_ref), channel_id=1, source_target_pairs={{0,4},{4,8},{8,12},{12,16},{16,20},{20,24},{24,28},{1,5},{5,9},{9,... | collective-permute-start | bytes 2359304 | tf_op jit(solution)/shard_map/ppermute | solution.py:310
  36.2 2.4 %collective-permute-start.3 = (bf16[3,512,256]{2,1,0:T(8,128)(2,1)S(1)}, bf16[3,512,256]{2,1,0:T(8,128)(2,1)}, u32[]{:S(2)}, u32[]{:S(2)}) collective-permute-start(bf16[3,512,256]{2,1,0:T(8,128)(2,1)S(1)} %pad_maximum_fusion.mid_ref), channel_id=1, source_target_pairs={{4,0},{8,4},{12,8},{16,12},{20,16},{24,20},{28,24},{5,1},{9,5},{13... | collective-permute-start | bytes 2359304 | tf_op jit(solution)/shard_map/ppermute | solution.py:311
  38.5 0.0 copy-done.21
  38.6 1.3 collective-permute-start.4
  39.9 1.2 collective-permute-start.5
  41.0 1.2 constant_dynamic-slice_fusion
  42.2 0.0 copy-done.18
  42.2 1.8 %collective-permute-start.10 = (bf16[64,2048]{1,0:T(8,128)(2,1)}, bf16[64,2048]{1,0:T(8,128)(2,1)S(1)}, u32[]{:S(2)}, u32[]{:S(2)}) collective-permute-start(bf16[64,2048]{1,0:T(8,128)(2,1)} %get-tuple-element.36), channel_id=1, source_target_pairs={{0,12},{4,8},{8,4},{12,0},{16,28},{20,24},{24,20},{28,16},{1,13},{... | collective-permute-start | bytes 786440 | tf_op jit(solution)/shard_map/ppermute | solution.py:297
  44.0 0.0 collective-permute-done.4.low_ref
  44.0 1.3 collective-permute-start.11
  45.3 0.0 collective-permute-done.5.high_ref
  45.3 2.2 %collective-permute-start.12 = (bf16[64,2048]{1,0:T(8,128)(2,1)}, bf16[64,2048]{1,0:T(8,128)(2,1)S(1)}, u32[]{:S(2)}, u32[]{:S(2)}) collective-permute-start(bf16[64,2048]{1,0:T(8,128)(2,1)} %get-tuple-element.34), channel_id=1, source_target_pairs={{0,20},{4,16},{8,28},{12,24},{16,4},{20,0},{24,12},{28,8},{1,21},{... | collective-permute-start | bytes 786440 | tf_op jit(solution)/shard_map/ppermute | solution.py:297
  47.5 0.0 collective-permute-done.2.before_ref
  47.5 6.5 %collective-permute-start.13 = (bf16[64,2048]{1,0:T(8,128)(2,1)}, bf16[64,2048]{1,0:T(8,128)(2,1)S(1)}, u32[]{:S(2)}, u32[]{:S(2)}) collective-permute-start(bf16[64,2048]{1,0:T(8,128)(2,1)} %get-tuple-element.40), channel_id=1, source_target_pairs={{0,24},{4,28},{8,16},{12,20},{16,8},{20,12},{24,0},{28,4},{1,25},{... | collective-permute-start | bytes 786440 | tf_op jit(solution)/shard_map/ppermute | solution.py:297
  54.7 0.0 copy-done.19
  54.7 0.0 copy-done.20
  54.7 2.8 %candidates.1 = (f32[9,256]{1,0:T(8,128)}, f32[9,256]{1,0:T(8,128)}) custom-call(s32[1,1]{1,0:T(1,128)S(6)} %copy.9.count_ref, s32[8,1024]{1,0:T(8,128)} %bitcast.15, s32[1,1024]{1,0:T(1,128)} %bitcast.17, bf16[2,2048]{1,0:T(2,128)(2,1)} %copy-done.19, bf16[2,2048]{1,0:T(2,128)(2,1)} %copy-done.18, bf16[2,2048]{1,0:T(2,128)(2,1)} %copy-done.20), custom_call_target="tpu_custom_call" | custom-call | tf_op jit(solution)/shard_map/candidates/pallas_call | solution.py:87
  57.5 0.0 collective-permute-done.3.after_ref
  57.5 0.0 collective-permute-start.14
  57.5 9.5 %transform.1 = (bf16[256,512]{1,0:T(8,128)(2,1)}, bf16[256,512]{1,0:T(8,128)(2,1)}) custom-call(bf16[3,512,256]{2,1,0:T(8,128)(2,1)} %collective-permute-done.2.before_ref, bf16[3,512,256]{2,1,0:T(8,128)(2,1)} %copy-done.1, bf16[3,512,256]{2,1,0:T(8,128)(2,1)} %collective-permute-done.3.after_ref, f32[9,256]{1,0:T(8,128)} %get-tuple-element.19.w_ref, ...), custom_call_target="tpu_custom_call" | custom-call | tf_op jit(solution)/shard_map/transform/pallas_call | solution.py:156
  67.0 0.0 collective-permute-done.10.refs_3_
  67.0 0.9 collective-permute-start.8
  67.9 0.0 collective-permute-done.11.refs_4_
  67.9 3.5 %collective-permute-start.9 = (bf16[64,2048]{1,0:T(8,128)(2,1)S(1)}, bf16[64,2048]{1,0:T(8,128)(2,1)S(1)}, u32[]{:S(2)}, u32[]{:S(2)}) collective-permute-start(bf16[64,2048]{1,0:T(8,128)(2,1)S(1)} %get-tuple-element.37), channel_id=1, source_target_pairs={{0,8},{4,12},{8,0},{12,4},{16,24},{20,28},{24,16},{28,20},{1,9},{5... | collective-permute-start | bytes 786440 | tf_op jit(solution)/shard_map/ppermute | solution.py:297
  71.4 6.3 %collective-permute-done.12.refs_5_ = bf16[64,2048]{1,0:T(8,128)(2,1)S(1)} collective-permute-done((bf16[64,2048]{1,0:T(8,128)(2,1)}, bf16[64,2048]{1,0:T(8,128)(2,1)S(1)}, u32[]{:S(2)}, u32[]{:S(2)}) %collective-permute-start.12) | collective-permute-done | bytes 262176 | tf_op jit(solution)/shard_map/ppermute | solution.py:297
  77.8 0.8 collective-permute-start.7
  78.5 9.3 %collective-permute-done.13.refs_6_ = bf16[64,2048]{1,0:T(8,128)(2,1)S(1)} collective-permute-done((bf16[64,2048]{1,0:T(8,128)(2,1)}, bf16[64,2048]{1,0:T(8,128)(2,1)S(1)}, u32[]{:S(2)}, u32[]{:S(2)}) %collective-permute-start.13) | collective-permute-done | bytes 262176 | tf_op jit(solution)/shard_map/ppermute | solution.py:297
  87.9 0.3 collective-permute-start.6
  88.2 6.6 %collective-permute-done.14.refs_7_ = bf16[64,2048]{1,0:T(8,128)(2,1)S(1)} collective-permute-done((bf16[64,2048]{1,0:T(8,128)(2,1)}, bf16[64,2048]{1,0:T(8,128)(2,1)S(1)}, u32[]{:S(2)}, u32[]{:S(2)}) %collective-permute-start.14) | collective-permute-done | bytes 262176 | tf_op jit(solution)/shard_map/ppermute | solution.py:297
  94.7 0.0 collective-permute-done.8.refs_1_
  94.8 0.0 collective-permute-done.9.refs_2_
  94.8 0.0 collective-permute-done.7.we_ref
  94.8 0.6 copy-done.6
  95.5 0.1 copy-done.8
  95.6 0.1 copy-done.11
  95.7 0.1 copy-done.15
  95.7 5.4 %far_update.1 = (f32[1,2048]{1,0:T(1,128)}, bf16[512,2048]{1,0:T(8,128)(2,1)}, bf16[64,2048]{1,0:T(8,128)(2,1)}, bf16[64,2048]{1,0:T(8,128)(2,1)}, bf16[64,2048]{1,0:T(8,128)(2,1)}, /*index=5*/bf16[64,2048]{1,0:T(8,128)(2,1)}) custom-call(bf16[256,512]{1,0:T(8,128)(2,1)} %get-tuple-element.22.wt_ref, bf16[256,512]{1,0:T(8,128)(2,1)} %copy-done.15, ...), custom_call_target="tpu_custom_call" | custom-call | tf_op jit(solution)/shard_map/far_update/pallas_call | solution.py:211
  101.2 0.0 collective-permute-done.6.we_ref
  101.2 0.7 copy-done.14
  101.9 4.0 %near_update.1 = (bf16[64,2048]{1,0:T(8,128)(2,1)}, bf16[64,2048]{1,0:T(8,128)(2,1)}, bf16[64,2048]{1,0:T(8,128)(2,1)}, bf16[64,2048]{1,0:T(8,128)(2,1)}) custom-call(bf16[256,512]{1,0:T(8,128)(2,1)} %get-tuple-element.21.wt_ref, bf16[256,512]{1,0:T(8,128)(2,1)} %copy-done.14, s32[1,2048]{1,0:T(1,128)} %bitcast.14, f32[1,2048]{1,0:T(1,128)} %get-tuple-element.23.xbar_ref, ...), custom_call_target="tpu_custom_call" | custom-call | tf_op jit(solution)/shard_map/near_update/pallas_call | solution.py:236
  105.9 0.0 collective-permute-start.15
  105.9 0.0 collective-permute-start.16
  105.9 2.1 %collective-permute-start.17 = (bf16[64,2048]{1,0:T(8,128)(2,1)}, bf16[64,2048]{1,0:T(8,128)(2,1)S(1)}, u32[]{:S(2)}, u32[]{:S(2)}) collective-permute-start(bf16[64,2048]{1,0:T(8,128)(2,1)} %get-tuple-element.28), channel_id=1, source_target_pairs={{0,12},{4,8},{8,4},{12,0},{16,28},{20,24},{24,20},{28,16},{1,13},{... | collective-permute-start | bytes 786440 | tf_op jit(solution)/shard_map/ppermute | solution.py:297
  108.1 0.0 collective-permute-start.18
  108.1 2.2 %collective-permute-start.19 = (bf16[64,2048]{1,0:T(8,128)(2,1)S(1)}, bf16[64,2048]{1,0:T(8,128)(2,1)S(1)}, u32[]{:S(2)}, u32[]{:S(2)}) collective-permute-start(bf16[64,2048]{1,0:T(8,128)(2,1)S(1)} %copy-done.25), channel_id=1, source_target_pairs={{0,20},{4,16},{8,28},{12,24},{16,4},{20,0},{24,12},{28,8},{1,21},{... | collective-permute-start | bytes 786440 | tf_op jit(solution)/shard_map/ppermute | solution.py:297
  110.3 0.0 collective-permute-done.15.refs_1_
  110.3 0.1 collective-permute-start.20
  110.4 10.7 %collective-permute-done.16.refs_2_ = bf16[64,2048]{1,0:T(8,128)(2,1)S(1)} collective-permute-done((bf16[64,2048]{1,0:T(8,128)(2,1)}, bf16[64,2048]{1,0:T(8,128)(2,1)S(1)}, u32[]{:S(2)}, u32[]{:S(2)}) %collective-permute-start.16) | collective-permute-done | bytes 262176 | tf_op jit(solution)/shard_map/ppermute | solution.py:297
  121.1 2.2 %collective-permute-start.21 = (bf16[64,2048]{1,0:T(8,128)(2,1)S(1)}, bf16[64,2048]{1,0:T(8,128)(2,1)S(1)}, u32[]{:S(2)}, u32[]{:S(2)}) collective-permute-start(bf16[64,2048]{1,0:T(8,128)(2,1)S(1)} %copy-done.23), channel_id=1, source_target_pairs={{0,28},{4,24},{8,20},{12,16},{16,12},{20,8},{24,4},{28,0},{1,29},{... | collective-permute-start | bytes 786440 | tf_op jit(solution)/shard_map/ppermute | solution.py:297
  123.2 3.5 %collective-permute-done.17.refs_3_ = bf16[64,2048]{1,0:T(8,128)(2,1)S(1)} collective-permute-done((bf16[64,2048]{1,0:T(8,128)(2,1)}, bf16[64,2048]{1,0:T(8,128)(2,1)S(1)}, u32[]{:S(2)}, u32[]{:S(2)}) %collective-permute-start.17) | collective-permute-done | bytes 262176 | tf_op jit(solution)/shard_map/ppermute | solution.py:297
  126.7 0.0 collective-permute-done.18.refs_4_
  126.7 15.5 %collective-permute-done.19.refs_5_ = bf16[64,2048]{1,0:T(8,128)(2,1)S(1)} collective-permute-done((bf16[64,2048]{1,0:T(8,128)(2,1)S(1)}, bf16[64,2048]{1,0:T(8,128)(2,1)S(1)}, u32[]{:S(2)}, u32[]{:S(2)}) %collective-permute-start.19) | collective-permute-done | bytes 262176 | tf_op jit(solution)/shard_map/ppermute | solution.py:297
  142.2 6.5 %collective-permute-done.20.refs_6_ = bf16[64,2048]{1,0:T(8,128)(2,1)S(1)} collective-permute-done((bf16[64,2048]{1,0:T(8,128)(2,1)S(1)}, bf16[64,2048]{1,0:T(8,128)(2,1)S(1)}, u32[]{:S(2)}, u32[]{:S(2)}) %collective-permute-start.20) | collective-permute-done | bytes 262176 | tf_op jit(solution)/shard_map/ppermute | solution.py:297
  148.7 6.2 %collective-permute-done.21.refs_7_ = bf16[64,2048]{1,0:T(8,128)(2,1)S(1)} collective-permute-done((bf16[64,2048]{1,0:T(8,128)(2,1)S(1)}, bf16[64,2048]{1,0:T(8,128)(2,1)S(1)}, u32[]{:S(2)}, u32[]{:S(2)}) %collective-permute-start.21) | collective-permute-done | bytes 262176 | tf_op jit(solution)/shard_map/ppermute | solution.py:297
  154.9 0.7 copy-done.17
  155.6 2.9 %assemble.1 = bf16[64,16384]{1,0:T(8,128)(2,1)} custom-call(bf16[64,2048]{1,0:T(8,128)(2,1)} %get-tuple-element.25.refs_0_, bf16[64,2048]{1,0:T(8,128)(2,1)} %copy-done.7, bf16[64,2048]{1,0:T(8,128)(2,1)} %copy-done.9, bf16[64,2048]{1,0:T(8,128)(2,1)} %copy-done.10, bf16[64,2048]{1,0:T(8,128)(2,1)} %copy-done.12, bf16[64,2048]{1,0:T(8,128)(2,1)} %copy-done.13, ...), custom_call_target="tpu_custom_call" | custom-call | tf_op jit(solution)/shard_map/assemble/pallas_call | solution.py:261
  (46 shorter events, 0.1 us)
Async XLA Ops:
  0.0 38.5 %copy-start.21 = (bf16[2048]{0:T(1024)(128)(2,1)S(1)}, bf16[2048]{0:T(1024)(128)(2,1)}, u32[]{:S(2)}) copy-start(bf16[2048]{0:T(1024)(128)(2,1)} %param.9) | copy-start | bytes 12292
  0.0 38.6 %copy-start.22 = (bf16[2048]{0:T(1024)(128)(2,1)S(1)}, bf16[2048]{0:T(1024)(128)(2,1)}, u32[]{:S(2)}) copy-start(bf16[2048]{0:T(1024)(128)(2,1)} %param.10) | copy-start | bytes 12292
  0.0 41.0 %copy-start = (bf16[64,16384]{1,0:T(8,128)(2,1)S(1)}, bf16[64,16384]{1,0:T(8,128)(2,1)}, u32[]{:S(2)}) copy-start(bf16[64,16384]{1,0:T(8,128)(2,1)} %x_ref.1) | copy-start | bytes 6291460
  19.3 7.7 %collective-permute-start = (bf16[512,256]{1,0:T(8,128)(2,1)S(1)}, bf16[512,256]{1,0:T(8,128)(2,1)S(1)}, u32[]{:S(2)}, u32[]{:S(2)}) collective-permute-start(bf16[512,256]{1,0:T(8,128)(2,1)S(1)} %bitcast.8), channel_id=1, source_target_pairs={{0,1},{1,2},{2,3},{3,0},{4,5},{5,6},{6,7},{7,4},{8,9},{9,10},{10,1... | collective-permute-start | bytes 786440 | tf_op jit(solution)/shard_map/ppermute | solution.py:307
  20.5 12.2 %collective-permute-start.1 = (bf16[512,256]{1,0:T(8,128)(2,1)S(1)}, bf16[512,256]{1,0:T(8,128)(2,1)S(1)}, u32[]{:S(2)}, u32[]{:S(2)}) collective-permute-start(bf16[512,256]{1,0:T(8,128)(2,1)S(1)} %bitcast.9), channel_id=1, source_target_pairs={{1,0},{2,1},{3,2},{0,3},{5,4},{6,5},{7,6},{4,7},{9,8},{10,9},{11,1... | collective-permute-start | bytes 786440 | tf_op jit(solution)/shard_map/ppermute | solution.py:308
  32.8 9.4 %copy-start.1 = (bf16[3,512,256]{2,1,0:T(8,128)(2,1)}, bf16[3,512,256]{2,1,0:T(8,128)(2,1)S(1)}, u32[]{:S(2)}) copy-start(bf16[3,512,256]{2,1,0:T(8,128)(2,1)S(1)} %pad_maximum_fusion.mid_ref) | copy-start | bytes 2359300
  32.8 14.8 %collective-permute-start.2 = (bf16[3,512,256]{2,1,0:T(8,128)(2,1)S(1)}, bf16[3,512,256]{2,1,0:T(8,128)(2,1)}, u32[]{:S(2)}, u32[]{:S(2)}) collective-permute-start(bf16[3,512,256]{2,1,0:T(8,128)(2,1)S(1)} %pad_maximum_fusion.mid_ref), channel_id=1, source_target_pairs={{0,4},{4,8},{8,12},{12,16},{16,20},{20,24},{24,28},{1,5},{5,9},{9,... | collective-permute-start | bytes 2359304 | tf_op jit(solution)/shard_map/ppermute | solution.py:310
  36.2 21.4 %collective-permute-start.3 = (bf16[3,512,256]{2,1,0:T(8,128)(2,1)S(1)}, bf16[3,512,256]{2,1,0:T(8,128)(2,1)}, u32[]{:S(2)}, u32[]{:S(2)}) collective-permute-start(bf16[3,512,256]{2,1,0:T(8,128)(2,1)S(1)} %pad_maximum_fusion.mid_ref), channel_id=1, source_target_pairs={{4,0},{8,4},{12,8},{16,12},{20,16},{24,20},{28,24},{5,1},{9,5},{13... | collective-permute-start | bytes 2359304 | tf_op jit(solution)/shard_map/ppermute | solution.py:311
  38.6 3.6 %copy-start.18 = (bf16[2,2048]{1,0:T(2,128)(2,1)}, bf16[2,2048]{1,0:T(2,128)(2,1)S(1)}, u32[]{:S(2)}) copy-start(bf16[2,2048]{1,0:T(2,128)(2,1)S(1)} %pad_maximum_fusion.1.own_ref) | copy-start | bytes 24580
  38.6 5.4 %collective-permute-start.4 = (bf16[2,2048]{1,0:T(2,128)(2,1)S(1)}, bf16[2,2048]{1,0:T(2,128)(2,1)S(1)}, u32[]{:S(2)}, u32[]{:S(2)}) collective-permute-start(bf16[2,2048]{1,0:T(2,128)(2,1)S(1)} %pad_maximum_fusion.1.own_ref), channel_id=1, source_target_pairs={{0,1},{1,2},{2,3},{3,0},{4,5},{5,6},{6,7},{7,4},{8,9},{9,10},{10,1... | collective-permute-start | bytes 24584 | tf_op jit(solution)/shard_map/ppermute | solution.py:301
  39.9 5.4 %collective-permute-start.5 = (bf16[2,2048]{1,0:T(2,128)(2,1)S(1)}, bf16[2,2048]{1,0:T(2,128)(2,1)S(1)}, u32[]{:S(2)}, u32[]{:S(2)}) collective-permute-start(bf16[2,2048]{1,0:T(2,128)(2,1)S(1)} %pad_maximum_fusion.1.own_ref), channel_id=1, source_target_pairs={{1,0},{2,1},{3,2},{0,3},{5,4},{6,5},{7,6},{4,7},{9,8},{10,9},{11,1... | collective-permute-start | bytes 24584 | tf_op jit(solution)/shard_map/ppermute | solution.py:302
  42.2 24.8 %collective-permute-start.10 = (bf16[64,2048]{1,0:T(8,128)(2,1)}, bf16[64,2048]{1,0:T(8,128)(2,1)S(1)}, u32[]{:S(2)}, u32[]{:S(2)}) collective-permute-start(bf16[64,2048]{1,0:T(8,128)(2,1)} %get-tuple-element.36), channel_id=1, source_target_pairs={{0,12},{4,8},{8,4},{12,0},{16,28},{20,24},{24,20},{28,16},{1,13},{... | collective-permute-start | bytes 786440 | tf_op jit(solution)/shard_map/ppermute | solution.py:297
  44.0 10.7 %copy-start.19 = (bf16[2,2048]{1,0:T(2,128)(2,1)}, bf16[2,2048]{1,0:T(2,128)(2,1)S(1)}, u32[]{:S(2)}) copy-start(bf16[2,2048]{1,0:T(2,128)(2,1)S(1)} %collective-permute-done.4.low_ref) | copy-start | bytes 24580
  44.0 23.9 %collective-permute-start.11 = (bf16[64,2048]{1,0:T(8,128)(2,1)}, bf16[64,2048]{1,0:T(8,128)(2,1)S(1)}, u32[]{:S(2)}, u32[]{:S(2)}) collective-permute-start(bf16[64,2048]{1,0:T(8,128)(2,1)} %get-tuple-element.35), channel_id=1, source_target_pairs={{0,16},{4,20},{8,24},{12,28},{16,0},{20,4},{24,8},{28,12},{1,17},{... | collective-permute-start | bytes 786440 | tf_op jit(solution)/shard_map/ppermute | solution.py:297
  45.3 9.4 %copy-start.20 = (bf16[2,2048]{1,0:T(2,128)(2,1)}, bf16[2,2048]{1,0:T(2,128)(2,1)S(1)}, u32[]{:S(2)}) copy-start(bf16[2,2048]{1,0:T(2,128)(2,1)S(1)} %collective-permute-done.5.high_ref) | copy-start | bytes 24580
  45.3 32.4 %collective-permute-start.12 = (bf16[64,2048]{1,0:T(8,128)(2,1)}, bf16[64,2048]{1,0:T(8,128)(2,1)S(1)}, u32[]{:S(2)}, u32[]{:S(2)}) collective-permute-start(bf16[64,2048]{1,0:T(8,128)(2,1)} %get-tuple-element.34), channel_id=1, source_target_pairs={{0,20},{4,16},{8,28},{12,24},{16,4},{20,0},{24,12},{28,8},{1,21},{... | collective-permute-start | bytes 786440 | tf_op jit(solution)/shard_map/ppermute | solution.py:297
  47.5 40.3 %collective-permute-start.13 = (bf16[64,2048]{1,0:T(8,128)(2,1)}, bf16[64,2048]{1,0:T(8,128)(2,1)S(1)}, u32[]{:S(2)}, u32[]{:S(2)}) collective-permute-start(bf16[64,2048]{1,0:T(8,128)(2,1)} %get-tuple-element.40), channel_id=1, source_target_pairs={{0,24},{4,28},{8,16},{12,20},{16,8},{20,12},{24,0},{28,4},{1,25},{... | collective-permute-start | bytes 786440 | tf_op jit(solution)/shard_map/ppermute | solution.py:297
  57.5 37.2 %collective-permute-start.14 = (bf16[64,2048]{1,0:T(8,128)(2,1)}, bf16[64,2048]{1,0:T(8,128)(2,1)S(1)}, u32[]{:S(2)}, u32[]{:S(2)}) collective-permute-start(bf16[64,2048]{1,0:T(8,128)(2,1)} %get-tuple-element.33), channel_id=1, source_target_pairs={{0,28},{4,24},{8,20},{12,16},{16,12},{20,8},{24,4},{28,0},{1,29},{... | collective-permute-start | bytes 786440 | tf_op jit(solution)/shard_map/ppermute | solution.py:297
  67.0 27.8 %copy-start.2 = (bf16[64,2048]{1,0:T(8,128)(2,1)}, bf16[64,2048]{1,0:T(8,128)(2,1)S(1)}, u32[]{:S(2)}) copy-start(bf16[64,2048]{1,0:T(8,128)(2,1)S(1)} %collective-permute-done.10.refs_3_) | copy-start | bytes 786436
  67.0 27.7 %collective-permute-start.8 = (bf16[64,2048]{1,0:T(8,128)(2,1)S(1)}, bf16[64,2048]{1,0:T(8,128)(2,1)S(1)}, u32[]{:S(2)}, u32[]{:S(2)}) collective-permute-start(bf16[64,2048]{1,0:T(8,128)(2,1)S(1)} %get-tuple-element.38), channel_id=1, source_target_pairs={{0,4},{4,0},{8,12},{12,8},{16,20},{20,16},{24,28},{28,24},{1,5},{5... | collective-permute-start | bytes 786440 | tf_op jit(solution)/shard_map/ppermute | solution.py:297
  67.9 26.9 %copy-start.3 = (bf16[64,2048]{1,0:T(8,128)(2,1)}, bf16[64,2048]{1,0:T(8,128)(2,1)S(1)}, u32[]{:S(2)}) copy-start(bf16[64,2048]{1,0:T(8,128)(2,1)S(1)} %collective-permute-done.11.refs_4_) | copy-start | bytes 786436
  67.9 26.8 %collective-permute-start.9 = (bf16[64,2048]{1,0:T(8,128)(2,1)S(1)}, bf16[64,2048]{1,0:T(8,128)(2,1)S(1)}, u32[]{:S(2)}, u32[]{:S(2)}) collective-permute-start(bf16[64,2048]{1,0:T(8,128)(2,1)S(1)} %get-tuple-element.37), channel_id=1, source_target_pairs={{0,8},{4,12},{8,0},{12,4},{16,24},{20,28},{24,16},{28,20},{1,9},{5... | collective-permute-start | bytes 786440 | tf_op jit(solution)/shard_map/ppermute | solution.py:297
  77.8 17.1 %copy-start.4 = (bf16[64,2048]{1,0:T(8,128)(2,1)}, bf16[64,2048]{1,0:T(8,128)(2,1)S(1)}, u32[]{:S(2)}) copy-start(bf16[64,2048]{1,0:T(8,128)(2,1)S(1)} %collective-permute-done.12.refs_5_) | copy-start | bytes 786436
  77.8 17.0 %collective-permute-start.7 = (bf16[256,512]{1,0:T(8,128)(2,1)}, bf16[256,512]{1,0:T(8,128)(2,1)S(1)}, u32[]{:S(2)}, u32[]{:S(2)}) collective-permute-start(bf16[256,512]{1,0:T(8,128)(2,1)} %get-tuple-element.22.wt_ref), channel_id=1, source_target_pairs={{1,0},{2,1},{3,2},{0,3},{5,4},{6,5},{7,6},{4,7},{9,8},{10,9},{11,1... | collective-permute-start | bytes 786440 | tf_op jit(solution)/shard_map/ppermute | solution.py:316
  87.9 6.9 %copy-start.5 = (bf16[64,2048]{1,0:T(8,128)(2,1)}, bf16[64,2048]{1,0:T(8,128)(2,1)S(1)}, u32[]{:S(2)}) copy-start(bf16[64,2048]{1,0:T(8,128)(2,1)S(1)} %collective-permute-done.13.refs_6_) | copy-start | bytes 786436
  87.9 13.3 %collective-permute-start.6 = (bf16[256,512]{1,0:T(8,128)(2,1)}, bf16[256,512]{1,0:T(8,128)(2,1)S(1)}, u32[]{:S(2)}, u32[]{:S(2)}) collective-permute-start(bf16[256,512]{1,0:T(8,128)(2,1)} %get-tuple-element.21.wt_ref), channel_id=1, source_target_pairs={{1,0},{2,1},{3,2},{0,3},{5,4},{6,5},{7,6},{4,7},{9,8},{10,9},{11,1... | collective-permute-start | bytes 786440 | tf_op jit(solution)/shard_map/ppermute | solution.py:317
  94.7 0.7 copy-start.6
  94.7 0.8 copy-start.8
  94.8 0.9 copy-start.11
  94.8 0.9 copy-start.15
  101.2 6.9 %copy-start.26 = (bf16[64,2048]{1,0:T(8,128)(2,1)S(1)}, bf16[64,2048]{1,0:T(8,128)(2,1)}, u32[]{:S(2)}) copy-start(bf16[64,2048]{1,0:T(8,128)(2,1)} %get-tuple-element.29) | copy-start | bytes 786436
  101.2 6.9 %copy-start.25 = (bf16[64,2048]{1,0:T(8,128)(2,1)S(1)}, bf16[64,2048]{1,0:T(8,128)(2,1)}, u32[]{:S(2)}) copy-start(bf16[64,2048]{1,0:T(8,128)(2,1)} %get-tuple-element.30) | copy-start | bytes 786436
  101.2 9.1 %copy-start.24 = (bf16[64,2048]{1,0:T(8,128)(2,1)S(1)}, bf16[64,2048]{1,0:T(8,128)(2,1)}, u32[]{:S(2)}) copy-start(bf16[64,2048]{1,0:T(8,128)(2,1)} %get-tuple-element.31) | copy-start | bytes 786436
  101.2 19.9 %copy-start.23 = (bf16[64,2048]{1,0:T(8,128)(2,1)S(1)}, bf16[64,2048]{1,0:T(8,128)(2,1)}, u32[]{:S(2)}) copy-start(bf16[64,2048]{1,0:T(8,128)(2,1)} %get-tuple-element.32) | copy-start | bytes 786436
  101.2 0.7 copy-start.14
  105.9 4.4 %collective-permute-start.15 = (bf16[64,2048]{1,0:T(8,128)(2,1)}, bf16[64,2048]{1,0:T(8,128)(2,1)S(1)}, u32[]{:S(2)}, u32[]{:S(2)}) collective-permute-start(bf16[64,2048]{1,0:T(8,128)(2,1)} %get-tuple-element.26), channel_id=1, source_target_pairs={{0,4},{4,0},{8,12},{12,8},{16,20},{20,16},{24,28},{28,24},{1,5},{5... | collective-permute-start | bytes 786440 | tf_op jit(solution)/shard_map/ppermute | solution.py:297
  105.9 15.2 %collective-permute-start.16 = (bf16[64,2048]{1,0:T(8,128)(2,1)}, bf16[64,2048]{1,0:T(8,128)(2,1)S(1)}, u32[]{:S(2)}, u32[]{:S(2)}) collective-permute-start(bf16[64,2048]{1,0:T(8,128)(2,1)} %get-tuple-element.27), channel_id=1, source_target_pairs={{0,8},{4,12},{8,0},{12,4},{16,24},{20,28},{24,16},{28,20},{1,9},{5... | collective-permute-start | bytes 786440 | tf_op jit(solution)/shard_map/ppermute | solution.py:297
  105.9 20.8 %collective-permute-start.17 = (bf16[64,2048]{1,0:T(8,128)(2,1)}, bf16[64,2048]{1,0:T(8,128)(2,1)S(1)}, u32[]{:S(2)}, u32[]{:S(2)}) collective-permute-start(bf16[64,2048]{1,0:T(8,128)(2,1)} %get-tuple-element.28), channel_id=1, source_target_pairs={{0,12},{4,8},{8,4},{12,0},{16,28},{20,24},{24,20},{28,16},{1,13},{... | collective-permute-start | bytes 786440 | tf_op jit(solution)/shard_map/ppermute | solution.py:297
  108.1 18.6 %collective-permute-start.18 = (bf16[64,2048]{1,0:T(8,128)(2,1)S(1)}, bf16[64,2048]{1,0:T(8,128)(2,1)S(1)}, u32[]{:S(2)}, u32[]{:S(2)}) collective-permute-start(bf16[64,2048]{1,0:T(8,128)(2,1)S(1)} %copy-done.26), channel_id=1, source_target_pairs={{0,16},{4,20},{8,24},{12,28},{16,0},{20,4},{24,8},{28,12},{1,17},{... | collective-permute-start | bytes 786440 | tf_op jit(solution)/shard_map/ppermute | solution.py:297
  108.1 34.1 %collective-permute-start.19 = (bf16[64,2048]{1,0:T(8,128)(2,1)S(1)}, bf16[64,2048]{1,0:T(8,128)(2,1)S(1)}, u32[]{:S(2)}, u32[]{:S(2)}) collective-permute-start(bf16[64,2048]{1,0:T(8,128)(2,1)S(1)} %copy-done.25), channel_id=1, source_target_pairs={{0,20},{4,16},{8,28},{12,24},{16,4},{20,0},{24,12},{28,8},{1,21},{... | collective-permute-start | bytes 786440 | tf_op jit(solution)/shard_map/ppermute | solution.py:297
  110.3 44.6 %copy-start.7 = (bf16[64,2048]{1,0:T(8,128)(2,1)}, bf16[64,2048]{1,0:T(8,128)(2,1)S(1)}, u32[]{:S(2)}) copy-start(bf16[64,2048]{1,0:T(8,128)(2,1)S(1)} %collective-permute-done.15.refs_1_) | copy-start | bytes 786436
  110.3 38.4 %collective-permute-start.20 = (bf16[64,2048]{1,0:T(8,128)(2,1)S(1)}, bf16[64,2048]{1,0:T(8,128)(2,1)S(1)}, u32[]{:S(2)}, u32[]{:S(2)}) collective-permute-start(bf16[64,2048]{1,0:T(8,128)(2,1)S(1)} %copy-done.24), channel_id=1, source_target_pairs={{0,24},{4,28},{8,16},{12,20},{16,8},{20,12},{24,0},{28,4},{1,25},{... | collective-permute-start | bytes 786440 | tf_op jit(solution)/shard_map/ppermute | solution.py:297
  121.1 33.8 %copy-start.9 = (bf16[64,2048]{1,0:T(8,128)(2,1)}, bf16[64,2048]{1,0:T(8,128)(2,1)S(1)}, u32[]{:S(2)}) copy-start(bf16[64,2048]{1,0:T(8,128)(2,1)S(1)} %collective-permute-done.16.refs_2_) | copy-start | bytes 786436
  121.1 33.8 %collective-permute-start.21 = (bf16[64,2048]{1,0:T(8,128)(2,1)S(1)}, bf16[64,2048]{1,0:T(8,128)(2,1)S(1)}, u32[]{:S(2)}, u32[]{:S(2)}) collective-permute-start(bf16[64,2048]{1,0:T(8,128)(2,1)S(1)} %copy-done.23), channel_id=1, source_target_pairs={{0,28},{4,24},{8,20},{12,16},{16,12},{20,8},{24,4},{28,0},{1,29},{... | collective-permute-start | bytes 786440 | tf_op jit(solution)/shard_map/ppermute | solution.py:297
  126.7 28.2 %copy-start.10 = (bf16[64,2048]{1,0:T(8,128)(2,1)}, bf16[64,2048]{1,0:T(8,128)(2,1)S(1)}, u32[]{:S(2)}) copy-start(bf16[64,2048]{1,0:T(8,128)(2,1)S(1)} %collective-permute-done.17.refs_3_) | copy-start | bytes 786436
  126.7 28.2 %copy-start.12 = (bf16[64,2048]{1,0:T(8,128)(2,1)}, bf16[64,2048]{1,0:T(8,128)(2,1)S(1)}, u32[]{:S(2)}) copy-start(bf16[64,2048]{1,0:T(8,128)(2,1)S(1)} %collective-permute-done.18.refs_4_) | copy-start | bytes 786436
  142.2 12.7 %copy-start.13 = (bf16[64,2048]{1,0:T(8,128)(2,1)}, bf16[64,2048]{1,0:T(8,128)(2,1)S(1)}, u32[]{:S(2)}) copy-start(bf16[64,2048]{1,0:T(8,128)(2,1)S(1)} %collective-permute-done.19.refs_5_) | copy-start | bytes 786436
  148.7 6.2 %copy-start.16 = (bf16[64,2048]{1,0:T(8,128)(2,1)}, bf16[64,2048]{1,0:T(8,128)(2,1)S(1)}, u32[]{:S(2)}) copy-start(bf16[64,2048]{1,0:T(8,128)(2,1)S(1)} %collective-permute-done.20.refs_6_) | copy-start | bytes 786436
  154.9 0.7 copy-start.17
where the time goes:
time: 159 us
  waiting for transfers between devices  75.6 us (48%)
  starting transfers between devices  34.4 us (22%)
  Pallas kernels  31.2 us (20%)
  blocking collectives  12.7 us (8%)
  local copies, waits for them, and re-layouts  3.52 us (2%)
    ppermute x14, waiting for transfers between devices, trade(): lax.ppermute(value, 'member', [(i, partner(i, d, bands)) for i in range(b...  64.5 us
    ppermute x14, starting transfers between devices, trade(): lax.ppermute(value, 'member', [(i, partner(i, d, bands)) for i in range(b...  22.8 us
    all_to_all x1, blocking collectives, local(): lax.all_to_all(proj, 'member', split_axis=0, concat_axis=0, tiled=True)  12.7 us
    pallas_call x1, Pallas kernels, transform(): pl.pallas_call(functools.partial(transform_kernel, count), in_specs=[pl.B...  9.52 us
    pallas_call x1, Pallas kernels, gather_obs(): pl.pallas_call(gather_kernel, grid=(bands,), in_specs=[pl.BlockSpec((1, w...  6.57 us
    ppermute x1, waiting for transfers between devices, local(): high = lax.ppermute(own, 'region', west)  5.67 us
    pallas_call x1, Pallas kernels, far_update(): pl.pallas_call(functools.partial(far_kernel, count), in_specs=[pl.BlockSp...  5.44 us
    ppermute x1, waiting for transfers between devices, local(): low = lax.ppermute(own, 'region', east)  5.36 us
  transfers between devices with their start and end apart: 22, of which 10 were waited for; matrix products, arithmetic and copies ran while one was open for 1% of the time, Pallas kernels for 11%

commit v1 on v0

v1 whole, which is shorter than its diff:
```python
import functools

import jax
import jax.numpy as jnp
from jax import lax
from jax.experimental import pallas as pl
from jax.experimental.pallas import tpu as pltpu
from jax.sharding import PartitionSpec as P


ITERS = 6

VMEM = pltpu.MemorySpace.VMEM
GRANT = pltpu.CompilerParams(vmem_limit_bytes=20 * 2**20)


def nt_dot(a, b):
    return lax.dot_general(a, b, (((1,), (1,)), ((), ())), preferred_element_type=jnp.float32)


def partner(me, d, count):
    if count & (count - 1) == 0:
        return me ^ d
    return (me + d) % count


def twin(me):
    return me + 1 - 2 * (me % 2)


def neighbour(me):
    return me - 1 + 2 * (me % 2)


def source(me, d, count):
    if count & (count - 1) == 0:
        return me ^ d
    return (me + count - d) % count


def gather_kernel(width, line_ref, x_ref, out_ref):
    group, members, _ = out_ref.shape
    rows = x_ref.shape[1] // group
    chunks = rows // width
    for g in range(group):
        line = line_ref[:, g * width : (g + 1) * width] - (pl.program_id(0) * group + g) * rows
        chunk = line // width
        place = line - chunk * width
        hot = (lax.broadcasted_iota(jnp.int32, (width, width), 0) == place).astype(jnp.bfloat16)
        at = g * rows
        stack = jnp.concatenate([x_ref[:, at + c * width : at + (c + 1) * width] for c in range(chunks)], axis=0)
        picked = jnp.dot(stack, hot, preferred_element_type=jnp.float32)
        result = picked[:members]
        for c in range(1, chunks):
            result = jnp.where(chunk == c, picked[c * members : (c + 1) * members], result)
        out_ref[g] = result.astype(jnp.bfloat16)


def gather_obs(prior, line, bands):
    members, fine = prior.shape
    rows = fine // bands
    width = line.shape[0] // bands
    group = 2 if bands % 2 == 0 else 1
    return pl.pallas_call(
        functools.partial(gather_kernel, width),
        grid=(bands // group,),
        in_specs=[
            pl.BlockSpec((1, group * width), lambda b: (0, b)),
            pl.BlockSpec((members, group * rows), lambda b: (0, b)),
        ],
        out_specs=pl.BlockSpec((group, members, width), lambda b: (b, 0, 0)),
        out_shape=jax.ShapeDtypeStruct((bands, members, width), jnp.bfloat16),
        name="gather_obs",
        compiler_params=GRANT,
    )(line.reshape(1, -1), prior)


def candidate_kernel(bands, count_ref, lookup_ref, dist_ref, low_ref, own_ref, high_ref, w_ref, val_ref):
    me = lax.axis_index("member")
    slots = lookup_ref.shape[1]
    obs_tile = own_ref.shape[1]
    width = obs_tile // bands
    index = lookup_ref[pl.ds(me, 1), :]
    live = lax.broadcasted_iota(jnp.int32, (1, slots), 1) < count_ref[0, 0]
    denom = jnp.where(live, 2.0 + dist_ref[...].astype(jnp.float32), 0.0)
    denom = jnp.broadcast_to(denom, (8, slots)).astype(jnp.bfloat16)
    rows = lax.broadcasted_iota(jnp.int32, (width, slots), 0)
    for off, band in enumerate((me, twin(me), neighbour(me))):
        valid = jnp.logical_and(band >= 0, band < bands)
        start = pl.multiple_of(jnp.clip(band, 0, bands - 1) * width, width)
        for side, ref in enumerate((low_ref, own_ref, high_ref)):
            base = jnp.where(valid, side * obs_tile + band * width, -4 * obs_tile)
            hot = (rows == index - base).astype(jnp.bfloat16)
            total = nt_dot(denom, hot)[0:1]
            pair = ref[:, pl.ds(start, width)].astype(jnp.float32)
            named = total > 0.0
            weight = pair[1:2] * 2.0 / jnp.where(named, total, 1.0)
            j = off * 3 + side
            w_ref[j : j + 1, :] = jnp.where(named, weight, 0.0)
            val_ref[j : j + 1, :] = pair[0:1]


def candidates(count, lookup, dist, low, own, high, bands):
    width = own.shape[1] // bands
    shape = jax.ShapeDtypeStruct((9, width), jnp.float32)
    return pl.pallas_call(
        functools.partial(candidate_kernel, bands),
        in_specs=[pl.BlockSpec(memory_space=pltpu.MemorySpace.SMEM)] + [pl.BlockSpec(memory_space=VMEM)] * 5,
        out_specs=[pl.BlockSpec(memory_space=VMEM)] * 2,
        out_shape=[shape, shape],
        name="candidates",
        compiler_params=GRANT,
    )(count, lookup, dist, low, own, high)


def as_row(column, eye):
    return jnp.sum(jnp.where(eye, column, 0.0), axis=0, keepdims=True)


def eye_mask(members):
    row = lax.broadcasted_iota(jnp.int32, (members, members), 0)
    return row == lax.broadcasted_iota(jnp.int32, (members, members), 1)


def add_planes(planes, places, w_ref, val_ref, pert_ref, weighted_ref):
    members, width = planes[0].shape
    gvec = jnp.zeros((members, 1), jnp.float32)
    for at, (j, ref) in enumerate(zip(places, planes)):
        values = ref[...].astype(jnp.float32)
        ybar = jnp.mean(values, axis=0, keepdims=True)
        pert = (values - ybar).astype(jnp.bfloat16)
        weighted = pert.astype(jnp.float32) * w_ref[j : j + 1, :]
        gvec = gvec + jnp.sum(weighted * (val_ref[j : j + 1, :] - ybar), axis=1, keepdims=True)
        pert_ref[:, at * width : (at + 1) * width] = pert
        weighted_ref[:, at * width : (at + 1) * width] = weighted.astype(jnp.bfloat16)
    return nt_dot(weighted_ref[...], pert_ref[...]), gvec


def gram_kernel(places, *refs):
    planes, (w_ref, val_ref, gram_ref, gvec_ref, pert_ref, weighted_ref) = refs[:-6], refs[-6:]
    gram, gvec = add_planes(planes, places, w_ref, val_ref, pert_ref, weighted_ref)
    gram_ref[...] = gram
    gvec_ref[...] = as_row(gvec, eye_mask(gram.shape[0]))


def gram_part(planes, places, w, val):
    members, width = planes[0].shape
    return pl.pallas_call(
        functools.partial(gram_kernel, places),
        in_specs=[pl.BlockSpec(memory_space=VMEM)] * (len(planes) + 2),
        out_specs=[pl.BlockSpec(memory_space=VMEM)] * 2,
        out_shape=[
            jax.ShapeDtypeStruct((members, members), jnp.float32),
            jax.ShapeDtypeStruct((1, members), jnp.float32),
        ],
        scratch_shapes=[pltpu.VMEM((members, len(planes) * width), jnp.bfloat16)] * 2,
        name="gram_part",
        compiler_params=GRANT,
    )(*planes, w, val)


def transform_kernel(
    count, places, before_ref, after_ref, w_ref, val_ref, gram_ref, part_ref, near_ref, far_ref, pert_ref, weighted_ref, wt_ref
):
    members = wt_ref.shape[0]
    planes = (before_ref.at[0], before_ref.at[1], after_ref.at[0], after_ref.at[1])
    gram, gvec = add_planes(planes, places, w_ref, val_ref, pert_ref, weighted_ref)
    eye = eye_mask(members)
    amat = gram_ref[...] + gram + jnp.where(eye, members - 1.0, 0.0)
    norm = jnp.sqrt(jnp.sum(jnp.sum(amat * amat, axis=1, keepdims=True), axis=0, keepdims=True))
    zmat = (amat / norm).astype(jnp.bfloat16)
    ident = jnp.where(eye, 1.5, 0.0)

    def mm(a, b):
        return jnp.dot(a, b, preferred_element_type=jnp.float32)

    tmat = (ident - 0.5 * zmat.astype(jnp.float32)).astype(jnp.bfloat16)
    ymat = tmat
    zmat = mm(tmat, zmat).astype(jnp.bfloat16)
    for step in range(1, ITERS):
        tmat = (ident - 0.5 * mm(zmat, ymat)).astype(jnp.bfloat16)
        ymat = mm(ymat, tmat).astype(jnp.bfloat16)
        if step < ITERS - 1:
            zmat = mm(tmat, zmat).astype(jnp.bfloat16)
    isq = ymat.astype(jnp.float32) / jnp.sqrt(norm)
    once = jnp.sum(isq * (part_ref[...] + as_row(gvec, eye)), axis=1, keepdims=True)
    wbar = jnp.sum(isq * as_row(once, eye), axis=1, keepdims=True)
    wt_ref[...] = (jnp.sqrt(members - 1.0) * isq + as_row(wbar, eye)).astype(jnp.bfloat16)
    me = lax.axis_index("member")
    each = members // count
    half = count // 2
    for d in range(count):
        rows = wt_ref[pl.ds(pl.multiple_of(partner(me, d, count) * each, each), each), :]
        if d < half:
            near_ref[d * each : (d + 1) * each, :] = rows
        else:
            far_ref[(d - half) * each : (d - half + 1) * each, :] = rows


def transform(before, after, places, w, val, gram, gvec, count):
    _, members, width = before.shape
    each = members // count
    half = count // 2
    return pl.pallas_call(
        functools.partial(transform_kernel, count, places),
        in_specs=[pl.BlockSpec(memory_space=VMEM)] * 6,
        out_specs=[pl.BlockSpec(memory_space=VMEM)] * 2,
        out_shape=[
            jax.ShapeDtypeStruct((half * each, members), jnp.bfloat16),
            jax.ShapeDtypeStruct(((count - half) * each, members), jnp.bfloat16),
        ],
        scratch_shapes=[
            pltpu.VMEM((members, len(places) * width), jnp.bfloat16),
            pltpu.VMEM((members, len(places) * width), jnp.bfloat16),
            pltpu.VMEM((members, members), jnp.bfloat16),
        ],
        name="transform",
        compiler_params=GRANT,
    )(before, after, w, val, gram, gvec)


def update_kernel(count, step, wt_ref, we_ref, level_ref, *refs):
    ins, outs, x_ref = refs[:count], refs[count:-1], refs[-1]
    me = lax.axis_index("member")
    each, rows = ins[1].shape
    members = each * count
    for d, ref in enumerate(ins):
        x_ref[pl.ds(pl.multiple_of(source(me, d, count) * each, each), each), :] = ref[...]
    own_sum = jnp.sum(wt_ref[...].astype(jnp.float32), axis=1, keepdims=True)
    east_sum = jnp.sum(we_ref[...].astype(jnp.float32), axis=1, keepdims=True)
    ones = jnp.ones((8, members), jnp.bfloat16)
    for at in range(0, rows, step):
        cols = slice(at, at + step)
        x = x_ref[:, cols]
        xbar = jnp.dot(ones, x, preferred_element_type=jnp.float32)[0:1] * (1.0 / members)
        own = jnp.dot(wt_ref[...], x, preferred_element_type=jnp.float32) - own_sum * xbar
        east = jnp.dot(we_ref[...], x, preferred_element_type=jnp.float32) - east_sum * xbar
        share = level_ref[:, cols].astype(jnp.float32) / 8.0
        result = (xbar + (1.0 - share) * own + share * east).astype(jnp.bfloat16)
        for place, out in enumerate(outs):
            out[:, cols] = result[place * each : (place + 1) * each]


def update(wt, we, level, blocks):
    count = len(blocks)
    each, rows = blocks[0].shape
    part = wt.shape[0] // each
    step = min(rows, 512)
    return pl.pallas_call(
        functools.partial(update_kernel, count, step),
        in_specs=[pl.BlockSpec(memory_space=VMEM)] * (3 + count),
        out_specs=[pl.BlockSpec(memory_space=VMEM)] * part,
        out_shape=[jax.ShapeDtypeStruct((each, rows), jnp.bfloat16)] * part,
        scratch_shapes=[pltpu.VMEM((each * count, rows), jnp.bfloat16)],
        compiler_params=GRANT,
    )(wt, we, level, *blocks)


def local(
    prior_states,
    measured_values,
    measurement_precision,
    measured_subgrid_line,
    neighbour_measurement_lookup,
    active_entries_tally,
    distance_tier,
    eastward_weight_share,
):
    bands = lax.axis_size("member")
    sectors = lax.axis_size("region")
    me = lax.axis_index("member")
    each, fine = prior_states.shape
    rows = fine // bands
    east = [(i, (i + 1) % sectors) for i in range(sectors)]
    west = [(target, origin) for origin, target in east]
    twins = [(i, twin(i)) for i in range(bands) if twin(i) < bands]
    other = [(i, neighbour(i)) for i in range(bands) if 0 <= neighbour(i) < bands]

    half = bands // 2

    def block_for(prior, d):
        return lax.dynamic_slice_in_dim(prior, partner(me, d, bands) * rows, rows, axis=1)

    def trade(value, d):
        return lax.ppermute(value, "member", [(i, partner(i, d, bands)) for i in range(bands)])

    def after(value, *others):
        return lax.optimization_barrier((value, *others))[0]

    first, middle, last = groups(bands)
    blocks = {d: block_for(prior_states, d) for d in first}
    states = {d: trade(blocks[d], d) for d in first}
    paired = jnp.stack((measured_values, measurement_precision))
    proj = gather_obs(prior_states, measured_subgrid_line, bands)
    prior_later = after(prior_states, proj)
    blocks.update({d: block_for(prior_later, d) for d in [0, *middle, *last]})
    own = lax.all_to_all(proj, "member", split_axis=0, concat_axis=0, tiled=True)
    own = own.reshape(each * bands, -1)
    pair_low = lax.ppermute(paired, "region", east)
    pair_high = lax.ppermute(paired, "region", west)
    states[0] = blocks[0]
    for d in middle:
        states[d] = trade(after(blocks[d], own), d)
    low = lax.ppermute(own, "region", east)
    high = lax.ppermute(own, "region", west)
    own_n = lax.ppermute(own, "member", other)
    own_t = lax.ppermute(own, "member", twins)
    sides = jnp.stack((low, high))
    sides_n = lax.ppermute(sides, "member", other)
    sides_t = lax.ppermute(sides, "member", twins)
    for d in last:
        states[d] = trade(after(blocks[d], sides_n, sides_t), d)
    w, val = candidates(
        active_entries_tally, neighbour_measurement_lookup[0], distance_tier[0], pair_low, paired, pair_high, bands
    )
    gram, gvec = gram_part((low, own, high, own_t, own_n), (0, 1, 2, 4, 7), w, val)
    wt_near, wt_far = transform(sides_t, sides_n, (3, 5, 6, 8), w, val, gram, gvec, bands)
    we_far = lax.ppermute(wt_far, "region", west)
    we_near = lax.ppermute(wt_near, "region", west)
    level = eastward_weight_share[0]
    ordered = [states[d] for d in range(bands)]
    far = update(wt_far, we_far, level, ordered)
    back = {d: trade(far[d - half], d) for d in range(half, bands)}
    near = update(wt_near, we_near, level, ordered)
    back[0] = near[0]
    for d in range(1, half):
        back[d] = trade(near[d], d)
    result = jnp.zeros((each, fine), jnp.bfloat16)
    for d in [0, *range(half, bands), *range(1, half)]:
        result = lax.dynamic_update_slice_in_dim(result, back[d], source(me, d, bands) * rows, axis=1)
    return result


def groups(bands):
    half = bands // 2
    quarter = max(half // 4, 1)
    far = list(range(half, bands))
    near = list(range(2, half))
    cut = len(near) // 2
    middle = far[quarter : 2 * quarter] + near[:cut] + list(range(1, min(2, half)))
    return far[:quarter], middle, far[2 * quarter :] + near[cut:]


def solution(mesh):
    in_specs = (
        P("member", "region"),
        P("region"),
        P("region"),
        P("region"),
        P("region", None, None),
        P("region", "member"),
        P("region", "member", None),
        P("region", "member", None),
    )
    out_specs = P("member", "region")
    return jax.shard_map(local, mesh=mesh, in_specs=in_specs, out_specs=out_specs, check_vma=False)
```

time: 159 us -> 140 us (0.88)
  the two profiles are of different devices: /device:TPU:9 before, /device:TPU:0 now
where the time goes in v1:
time: 140 us
  waiting for transfers between devices  68.2 us (49%)
  starting transfers between devices  32.7 us (23%)
  Pallas kernels  16.6 us (12%)
  blocking collectives  15.9 us (11%)
  local copies, waits for them, and re-layouts  4.54 us (3%)
    ppermute x14, waiting for transfers between devices, trade(): lax.ppermute(value, 'member', [(i, partner(i, d, bands)) for i in range(b...  58.4 us
    ppermute x14, starting transfers between devices, trade(): lax.ppermute(value, 'member', [(i, partner(i, d, bands)) for i in range(b...  18.7 us
    all_to_all x1, blocking collectives, local(): lax.all_to_all(proj, 'member', split_axis=0, concat_axis=0, tiled=True)  15.9 us
    pallas_call x1, Pallas kernels, transform(): pl.pallas_call(functools.partial(transform_kernel, count, places), in_spe...  7.35 us
    ppermute x1, waiting for transfers between devices, local(): low = lax.ppermute(own, 'region', east)  5.16 us
    pallas_call x2, Pallas kernels, update(): pl.pallas_call(functools.partial(update_kernel, count, step), in_specs=[p...  4.01 us
    ppermute x1, waiting for transfers between devices, local(): pair_low = lax.ppermute(paired, 'region', east)  3.04 us
    ppermute x1, starting transfers between devices, local(): pair_high = lax.ppermute(paired, 'region', west)  2.97 us
  transfers between devices with their start and end apart: 24, of which 9 were waited for; matrix products, arithmetic and copies ran while one was open for 2% of the time, Pallas kernels for 11%

profile of v1, /device:TPU:0, one launch (start us, length us, event | category | flops | bytes accessed | tf_op | source)
XLA Modules:
  0.0 139.7 jit_solution(1086471495742797416)
XLA Ops:
  0.0 1.6 %copy-done = bf16[64,16384]{1,0:T(8,128)(2,1)S(1)} copy-done((bf16[64,16384]{1,0:T(8,128)(2,1)S(1)}, bf16[64,16384]{1,0:T(8,128)(2,1)}, u32[]{:S(2)}) %copy-start) | copy-done | bytes 2097176
  1.6 0.7 copy-done.4
  2.3 1.4 %gather_obs.1 = bf16[8,64,256]{2,1,0:T(8,128)(2,1)S(1)} custom-call(s32[1,2048]{1,0:T(1,128)S(1)} %bitcast.17, bf16[64,16384]{1,0:T(8,128)(2,1)S(1)} %copy-done), custom_call_target="tpu_custom_call" | custom-call | tf_op jit(solution)/shard_map/gather_obs/pallas_call | solution.py:64
  3.8 15.9 %all_to_all.5 = bf16[8,64,256]{2,1,0:T(8,128)(2,1)S(1)} all-to-all(bf16[8,64,256]{2,1,0:T(8,128)(2,1)S(1)} %gather_obs.1), channel_id=1, replica_groups=mesh['member'=8,'region'=4] {'member'}, dimensions={0} | all-to-all | bytes 524288 | tf_op jit(solution)/shard_map/all_to_all | solution.py:297
  19.6 2.4 %collective-permute-start.1 = (bf16[512,256]{1,0:T(8,128)(2,1)S(1)}, bf16[512,256]{1,0:T(8,128)(2,1)S(1)}, u32[]{:S(2)}, u32[]{:S(2)}) collective-permute-start(bf16[512,256]{1,0:T(8,128)(2,1)S(1)} %bitcast.7), channel_id=1, source_target_pairs={{1,0},{2,1},{3,2},{0,3},{5,4},{6,5},{7,6},{4,7},{9,8},{10,9},{11,1... | collective-permute-start | bytes 786440 | tf_op jit(solution)/shard_map/ppermute | solution.py:305
  22.1 0.0 collective-permute-start
  22.1 3.0 %collective-permute-start.5 = (bf16[2,2048]{1,0:T(2,128)(2,1)S(1)}, bf16[2,2048]{1,0:T(2,128)(2,1)S(1)}, u32[]{:S(2)}, u32[]{:S(2)}) collective-permute-start(bf16[2,2048]{1,0:T(2,128)(2,1)S(1)} %pad_maximum_fusion.1.own_ref), channel_id=1, source_target_pairs={{1,0},{2,1},{3,2},{0,3},{5,4},{6,5},{7,6},{4,7},{9,8},{10,9},{11,1... | collective-permute-start | bytes 24584 | tf_op jit(solution)/shard_map/ppermute | solution.py:300
  25.1 0.7 collective-permute-start.7
  25.8 1.5 %collective-permute-start.6 = (bf16[512,256]{1,0:T(8,128)(2,1)S(1)}, bf16[512,256]{1,0:T(8,128)(2,1)}, u32[]{:S(2)}, u32[]{:S(2)}) collective-permute-start(bf16[512,256]{1,0:T(8,128)(2,1)S(1)} %bitcast.10), channel_id=1, source_target_pairs={{0,4},{4,0},{8,12},{12,8},{16,20},{20,16},{24,28},{28,24},{1,5},{5... | collective-permute-start | bytes 786440 | tf_op jit(solution)/shard_map/ppermute | solution.py:307
  27.3 1.5 %collective-permute-done.1.refs_2_ = bf16[512,256]{1,0:T(8,128)(2,1)S(1)} collective-permute-done((bf16[512,256]{1,0:T(8,128)(2,1)S(1)}, bf16[512,256]{1,0:T(8,128)(2,1)S(1)}, u32[]{:S(2)}, u32[]{:S(2)}) %collective-permute-start.1) | collective-permute-done | bytes 262176 | tf_op jit(solution)/shard_map/ppermute | solution.py:305
  28.8 5.2 %collective-permute-done.refs_0_ = bf16[512,256]{1,0:T(8,128)(2,1)S(1)} collective-permute-done((bf16[512,256]{1,0:T(8,128)(2,1)S(1)}, bf16[512,256]{1,0:T(8,128)(2,1)S(1)}, u32[]{:S(2)}, u32[]{:S(2)}) %collective-permute-start) | collective-permute-done | bytes 262176 | tf_op jit(solution)/shard_map/ppermute | solution.py:304
  34.0 0.8 pad_maximum_fusion
  34.8 1.6 %collective-permute-start.3 = (bf16[2,512,256]{2,1,0:T(8,128)(2,1)}, bf16[2,512,256]{2,1,0:T(8,128)(2,1)}, u32[]{:S(2)}, u32[]{:S(2)}) collective-permute-start(bf16[2,512,256]{2,1,0:T(8,128)(2,1)} %pad_maximum_fusion), channel_id=1, source_target_pairs={{4,8},{8,4},{12,16},{16,12},{20,24},{24,20},{5,9},{9,5},{13,17},{1... | collective-permute-start | bytes 1572872 | tf_op jit(solution)/shard_map/ppermute | solution.py:309
  36.4 0.7 collective-permute-start.2
  37.1 1.2 constant_dynamic-slice_fusion
  38.3 0.0 collective-permute-done.5.high_ref
  38.3 1.5 %collective-permute-start.4 = (bf16[2,2048]{1,0:T(2,128)(2,1)S(1)}, bf16[2,2048]{1,0:T(2,128)(2,1)S(1)}, u32[]{:S(2)}, u32[]{:S(2)}) collective-permute-start(bf16[2,2048]{1,0:T(2,128)(2,1)S(1)} %pad_maximum_fusion.1.own_ref), channel_id=1, source_target_pairs={{0,1},{1,2},{2,3},{3,0},{4,5},{5,6},{6,7},{7,4},{8,9},{9,10},{10,1... | collective-permute-start | bytes 24584 | tf_op jit(solution)/shard_map/ppermute | solution.py:299
  39.8 3.0 %collective-permute-done.4.low_ref = bf16[2,2048]{1,0:T(2,128)(2,1)S(1)} collective-permute-done((bf16[2,2048]{1,0:T(2,128)(2,1)S(1)}, bf16[2,2048]{1,0:T(2,128)(2,1)S(1)}, u32[]{:S(2)}, u32[]{:S(2)}) %collective-permute-start.4) | collective-permute-done | bytes 8224 | tf_op jit(solution)/shard_map/ppermute | solution.py:299
  42.9 2.4 %collective-permute-start.12 = (bf16[64,2048]{1,0:T(8,128)(2,1)S(1)}, bf16[64,2048]{1,0:T(8,128)(2,1)S(1)}, u32[]{:S(2)}, u32[]{:S(2)}) collective-permute-start(bf16[64,2048]{1,0:T(8,128)(2,1)S(1)} %constant_dynamic-slice_fusion.3), channel_id=1, source_target_pairs={{0,16},{4,20},{8,24},{12,28},{16,0},{20,4},{24,8},{28,12},{1,17},{... | collective-permute-start | bytes 786440 | tf_op jit(solution)/shard_map/ppermute | solution.py:285
  45.3 0.0 collective-permute-done.7.refs_4_
  45.3 0.0 collective-permute-start.9
  45.3 0.0 collective-permute-done.6.refs_3_
  45.3 0.1 collective-permute-start.10
  45.3 0.0 collective-permute-done.3.after_ref
  45.4 1.8 %collective-permute-start.13 = (bf16[64,2048]{1,0:T(8,128)(2,1)}, bf16[64,2048]{1,0:T(8,128)(2,1)S(1)}, u32[]{:S(2)}, u32[]{:S(2)}) collective-permute-start(bf16[64,2048]{1,0:T(8,128)(2,1)} %get-tuple-element.35), channel_id=1, source_target_pairs={{0,20},{4,16},{8,28},{12,24},{16,4},{20,0},{24,12},{28,8},{1,21},{... | collective-permute-start | bytes 786440 | tf_op jit(solution)/shard_map/ppermute | solution.py:285
  47.8 0.0 copy-done.3
  47.8 0.0 copy-done.5
  47.8 1.4 candidates.1
  49.1 2.4 %gram_part.1 = (f32[512,512]{1,0:T(8,128)S(1)}, f32[1,512]{1,0:T(1,128)S(1)}) custom-call(bf16[512,256]{1,0:T(8,128)(2,1)S(1)} %collective-permute-done.refs_0_, bf16[512,256]{1,0:T(8,128)(2,1)S(1)} %bitcast.11, bf16[512,256]{1,0:T(8,128)(2,1)S(1)} %collective-permute-done.1.refs_2_, bf16[512,256]{1,0:T(8,128)(2,1)} %collective-permute-done.6.refs_3_, ...), custom_call_target="tpu_custom_call" | custom-call | tf_op jit(solution)/shard_map/gram_part/pallas_call | solution.py:148
  51.6 0.0 collective-permute-done.2.before_ref
  51.6 7.3 %transform.1 = (bf16[256,512]{1,0:T(8,128)(2,1)S(1)}, bf16[256,512]{1,0:T(8,128)(2,1)S(1)}) custom-call(bf16[2,512,256]{2,1,0:T(8,128)(2,1)} %collective-permute-done.2.before_ref, bf16[2,512,256]{2,1,0:T(8,128)(2,1)} %collective-permute-done.3.after_ref, f32[9,256]{1,0:T(8,128)S(1)} %get-tuple-element.26.refs_5_.w_ref, ...), custom_call_target="tpu_custom_call" | custom-call | tf_op jit(solution)/shard_map/transform/pallas_call | solution.py:204
  58.9 2.0 %collective-permute-start.16 = (bf16[256,512]{1,0:T(8,128)(2,1)S(1)}, bf16[256,512]{1,0:T(8,128)(2,1)S(1)}, u32[]{:S(2)}, u32[]{:S(2)}) collective-permute-start(bf16[256,512]{1,0:T(8,128)(2,1)S(1)} %get-tuple-element.39.wt_ref), channel_id=1, source_target_pairs={{1,0},{2,1},{3,2},{0,3},{5,4},{6,5},{7,6},{4,7},{9,8},{10,9},{11,1... | collective-permute-start | bytes 786440 | tf_op jit(solution)/shard_map/ppermute | solution.py:318
  60.9 0.0 collective-permute-done.12.refs_4_
  60.9 1.6 %collective-permute-start.11 = (bf16[64,2048]{1,0:T(8,128)(2,1)S(1)}, bf16[64,2048]{1,0:T(8,128)(2,1)S(1)}, u32[]{:S(2)}, u32[]{:S(2)}) collective-permute-start(bf16[64,2048]{1,0:T(8,128)(2,1)S(1)} %copy-done.9), channel_id=1, source_target_pairs={{0,12},{4,8},{8,4},{12,0},{16,28},{20,24},{24,20},{28,16},{1,13},{... | collective-permute-start | bytes 786440 | tf_op jit(solution)/shard_map/ppermute | solution.py:285
  62.5 0.0 collective-permute-done.9.refs_1_
  62.5 0.1 collective-permute-start.14
  62.6 0.0 collective-permute-done.10.refs_2_
  62.6 0.7 collective-permute-start.15
  63.4 3.5 %collective-permute-done.13.refs_5_ = bf16[64,2048]{1,0:T(8,128)(2,1)S(1)} collective-permute-done((bf16[64,2048]{1,0:T(8,128)(2,1)}, bf16[64,2048]{1,0:T(8,128)(2,1)S(1)}, u32[]{:S(2)}, u32[]{:S(2)}) %collective-permute-start.13) | collective-permute-done | bytes 262176 | tf_op jit(solution)/shard_map/ppermute | solution.py:285
  66.8 0.7 collective-permute-start.8
  67.5 0.0 collective-permute-done.16.we_ref
  67.5 15.6 %collective-permute-done.11.refs_3_ = bf16[64,2048]{1,0:T(8,128)(2,1)S(1)} collective-permute-done((bf16[64,2048]{1,0:T(8,128)(2,1)S(1)}, bf16[64,2048]{1,0:T(8,128)(2,1)S(1)}, u32[]{:S(2)}, u32[]{:S(2)}) %collective-permute-start.11) | collective-permute-done | bytes 262176 | tf_op jit(solution)/shard_map/ppermute | solution.py:285
  83.1 0.0 collective-permute-done.14.refs_6_
  83.1 0.0 collective-permute-done.15.refs_7_
  83.1 2.0 %shard_map.83 = (bf16[64,2048]{1,0:T(8,128)(2,1)S(1)}, bf16[64,2048]{1,0:T(8,128)(2,1)S(1)}, bf16[64,2048]{1,0:T(8,128)(2,1)S(1)}, bf16[64,2048]{1,0:T(8,128)(2,1)S(1)}) custom-call(bf16[256,512]{1,0:T(8,128)(2,1)S(1)} %get-tuple-element.39.wt_ref, bf16[256,512]{1,0:T(8,128)(2,1)S(1)} %collective-permute-done.16.we_ref, s32[1,2048]{1,0:T(1,128)S(1)} %bitcast.14, ...), custom_call_target="tpu_custom_call" | custom-call | tf_op jit(solution)/shard_map/pallas_call | solution.py:249
  85.1 7.4 %collective-permute-start.17 = (bf16[64,2048]{1,0:T(8,128)(2,1)S(1)}, bf16[64,2048]{1,0:T(8,128)(2,1)S(1)}, u32[]{:S(2)}, u32[]{:S(2)}) collective-permute-start(bf16[64,2048]{1,0:T(8,128)(2,1)S(1)} %get-tuple-element.40), channel_id=1, source_target_pairs={{0,16},{4,20},{8,24},{12,28},{16,0},{20,4},{24,8},{28,12},{1,17},{... | collective-permute-start | bytes 786440 | tf_op jit(solution)/shard_map/ppermute | solution.py:285
  92.5 0.7 collective-permute-start.18
  93.2 1.6 %collective-permute-start.19 = (bf16[64,2048]{1,0:T(8,128)(2,1)S(1)}, bf16[64,2048]{1,0:T(8,128)(2,1)S(1)}, u32[]{:S(2)}, u32[]{:S(2)}) collective-permute-start(bf16[64,2048]{1,0:T(8,128)(2,1)S(1)} %get-tuple-element.42), channel_id=1, source_target_pairs={{0,24},{4,28},{8,16},{12,20},{16,8},{20,12},{24,0},{28,4},{1,25},{... | collective-permute-start | bytes 786440 | tf_op jit(solution)/shard_map/ppermute | solution.py:285
  94.7 1.6 %collective-permute-start.20 = (bf16[64,2048]{1,0:T(8,128)(2,1)S(1)}, bf16[64,2048]{1,0:T(8,128)(2,1)S(1)}, u32[]{:S(2)}, u32[]{:S(2)}) collective-permute-start(bf16[64,2048]{1,0:T(8,128)(2,1)S(1)} %get-tuple-element.43), channel_id=1, source_target_pairs={{0,28},{4,24},{8,20},{12,16},{16,12},{20,8},{24,4},{28,0},{1,29},{... | collective-permute-start | bytes 786440 | tf_op jit(solution)/shard_map/ppermute | solution.py:285
  96.4 0.0 collective-permute-done.8.we_ref
  96.4 2.0 %shard_map.82 = (bf16[64,2048]{1,0:T(8,128)(2,1)S(1)}, bf16[64,2048]{1,0:T(8,128)(2,1)S(1)}, bf16[64,2048]{1,0:T(8,128)(2,1)S(1)}, bf16[64,2048]{1,0:T(8,128)(2,1)S(1)}) custom-call(bf16[256,512]{1,0:T(8,128)(2,1)S(1)} %get-tuple-element.30.wt_ref, bf16[256,512]{1,0:T(8,128)(2,1)S(1)} %collective-permute-done.8.we_ref, s32[1,2048]{1,0:T(1,128)S(1)} %bitcast.15, ...), custom_call_target="tpu_custom_call" | custom-call | tf_op jit(solution)/shard_map/pallas_call | solution.py:249
  98.4 0.8 collective-permute-start.21
  99.2 0.1 broadcast_in_dim.3
  99.4 22.4 %collective-permute-done.17 = bf16[64,2048]{1,0:T(8,128)(2,1)S(1)} collective-permute-done((bf16[64,2048]{1,0:T(8,128)(2,1)S(1)}, bf16[64,2048]{1,0:T(8,128)(2,1)S(1)}, u32[]{:S(2)}, u32[]{:S(2)}) %collective-permute-start.17) | collective-permute-done | bytes 262176 | tf_op jit(solution)/shard_map/ppermute | solution.py:285
  121.8 0.0 collective-permute-start.22
  121.8 6.3 %collective-permute-done.18 = bf16[64,2048]{1,0:T(8,128)(2,1)S(1)} collective-permute-done((bf16[64,2048]{1,0:T(8,128)(2,1)S(1)}, bf16[64,2048]{1,0:T(8,128)(2,1)S(1)}, u32[]{:S(2)}, u32[]{:S(2)}) %collective-permute-start.18) | collective-permute-done | bytes 262176 | tf_op jit(solution)/shard_map/ppermute | solution.py:285
  128.1 0.0 collective-permute-start.23
  128.1 0.0 collective-permute-done.19
  128.2 0.0 collective-permute-done.20
  128.2 0.0 collective-permute-done.21
  128.3 5.2 %collective-permute-done.22 = bf16[64,2048]{1,0:T(8,128)(2,1)S(1)} collective-permute-done((bf16[64,2048]{1,0:T(8,128)(2,1)S(1)}, bf16[64,2048]{1,0:T(8,128)(2,1)S(1)}, u32[]{:S(2)}, u32[]{:S(2)}) %collective-permute-start.22) | collective-permute-done | bytes 262176 | tf_op jit(solution)/shard_map/ppermute | solution.py:285
  133.4 0.0 copy-start.6
  133.4 5.5 %collective-permute-done.23 = bf16[64,2048]{1,0:T(8,128)(2,1)S(1)} collective-permute-done((bf16[64,2048]{1,0:T(8,128)(2,1)S(1)}, bf16[64,2048]{1,0:T(8,128)(2,1)S(1)}, u32[]{:S(2)}, u32[]{:S(2)}) %collective-permute-start.23) | collective-permute-done | bytes 262176 | tf_op jit(solution)/shard_map/ppermute | solution.py:285
  138.9 0.7 constant_dynamic-update-slice_fusion
  (30 shorter events, 0.3 us)
Async XLA Ops:
  0.0 1.6 %copy-start = (bf16[64,16384]{1,0:T(8,128)(2,1)S(1)}, bf16[64,16384]{1,0:T(8,128)(2,1)}, u32[]{:S(2)}) copy-start(bf16[64,16384]{1,0:T(8,128)(2,1)} %x_ref.1) | copy-start | bytes 6291460
  1.6 0.7 copy-start.4
  2.3 19.8 %copy-start.10 = (bf16[2048]{0:T(1024)(128)(2,1)S(1)}, bf16[2048]{0:T(1024)(128)(2,1)}, u32[]{:S(2)}) copy-start(bf16[2048]{0:T(1024)(128)(2,1)} %param.9) | copy-start | bytes 12292
  2.3 19.8 %copy-start.11 = (bf16[2048]{0:T(1024)(128)(2,1)S(1)}, bf16[2048]{0:T(1024)(128)(2,1)}, u32[]{:S(2)}) copy-start(bf16[2048]{0:T(1024)(128)(2,1)} %param.10) | copy-start | bytes 12292
  2.3 34.8 %copy-start.1 = (bf16[64,16384]{1,0:T(8,128)(2,1)S(1)}, bf16[64,16384]{1,0:T(8,128)(2,1)}, u32[]{:S(2)}) copy-start(bf16[64,16384]{1,0:T(8,128)(2,1)} %x_ref.1) | copy-start | bytes 6291460
  19.6 9.2 %collective-permute-start.1 = (bf16[512,256]{1,0:T(8,128)(2,1)S(1)}, bf16[512,256]{1,0:T(8,128)(2,1)S(1)}, u32[]{:S(2)}, u32[]{:S(2)}) collective-permute-start(bf16[512,256]{1,0:T(8,128)(2,1)S(1)} %bitcast.7), channel_id=1, source_target_pairs={{1,0},{2,1},{3,2},{0,3},{5,4},{6,5},{7,6},{4,7},{9,8},{10,9},{11,1... | collective-permute-start | bytes 786440 | tf_op jit(solution)/shard_map/ppermute | solution.py:305
  22.1 11.9 %collective-permute-start = (bf16[512,256]{1,0:T(8,128)(2,1)S(1)}, bf16[512,256]{1,0:T(8,128)(2,1)S(1)}, u32[]{:S(2)}, u32[]{:S(2)}) collective-permute-start(bf16[512,256]{1,0:T(8,128)(2,1)S(1)} %bitcast.8), channel_id=1, source_target_pairs={{0,1},{1,2},{2,3},{3,0},{4,5},{5,6},{6,7},{7,4},{8,9},{9,10},{10,1... | collective-permute-start | bytes 786440 | tf_op jit(solution)/shard_map/ppermute | solution.py:304
  22.1 16.1 %collective-permute-start.5 = (bf16[2,2048]{1,0:T(2,128)(2,1)S(1)}, bf16[2,2048]{1,0:T(2,128)(2,1)S(1)}, u32[]{:S(2)}, u32[]{:S(2)}) collective-permute-start(bf16[2,2048]{1,0:T(2,128)(2,1)S(1)} %pad_maximum_fusion.1.own_ref), channel_id=1, source_target_pairs={{1,0},{2,1},{3,2},{0,3},{5,4},{6,5},{7,6},{4,7},{9,8},{10,9},{11,1... | collective-permute-start | bytes 24584 | tf_op jit(solution)/shard_map/ppermute | solution.py:300
  25.1 20.1 %collective-permute-start.7 = (bf16[512,256]{1,0:T(8,128)(2,1)S(1)}, bf16[512,256]{1,0:T(8,128)(2,1)S(1)}, u32[]{:S(2)}, u32[]{:S(2)}) collective-permute-start(bf16[512,256]{1,0:T(8,128)(2,1)S(1)} %bitcast.9), channel_id=1, source_target_pairs={{4,8},{8,4},{12,16},{16,12},{20,24},{24,20},{5,9},{9,5},{13,17},{1... | collective-permute-start | bytes 786440 | tf_op jit(solution)/shard_map/ppermute | solution.py:306
  25.8 19.5 %collective-permute-start.6 = (bf16[512,256]{1,0:T(8,128)(2,1)S(1)}, bf16[512,256]{1,0:T(8,128)(2,1)}, u32[]{:S(2)}, u32[]{:S(2)}) collective-permute-start(bf16[512,256]{1,0:T(8,128)(2,1)S(1)} %bitcast.10), channel_id=1, source_target_pairs={{0,4},{4,0},{8,12},{12,8},{16,20},{20,16},{24,28},{28,24},{1,5},{5... | collective-permute-start | bytes 786440 | tf_op jit(solution)/shard_map/ppermute | solution.py:307
  34.8 13.0 %copy-start.3 = (s32[1,8,1024]{2,1,0:T(8,128)S(1)}, s32[1,8,1024]{2,1,0:T(8,128)}, u32[]{:S(2)}) copy-start(s32[1,8,1024]{2,1,0:T(8,128)} %param.12) | copy-start | bytes 98308
  34.8 13.0 %copy-start.5 = (s32[1,1,1024]{2,1,0:T(1,128)S(1)}, s32[1,1,1024]{2,1,0:T(1,128)}, u32[]{:S(2)}) copy-start(s32[1,1,1024]{2,1,0:T(1,128)} %param.14) | copy-start | bytes 12292
  34.8 10.5 %collective-permute-start.3 = (bf16[2,512,256]{2,1,0:T(8,128)(2,1)}, bf16[2,512,256]{2,1,0:T(8,128)(2,1)}, u32[]{:S(2)}, u32[]{:S(2)}) collective-permute-start(bf16[2,512,256]{2,1,0:T(8,128)(2,1)} %pad_maximum_fusion), channel_id=1, source_target_pairs={{4,8},{8,4},{12,16},{16,12},{20,24},{24,20},{5,9},{9,5},{13,17},{1... | collective-permute-start | bytes 1572872 | tf_op jit(solution)/shard_map/ppermute | solution.py:309
  36.4 15.1 %collective-permute-start.2 = (bf16[2,512,256]{2,1,0:T(8,128)(2,1)}, bf16[2,512,256]{2,1,0:T(8,128)(2,1)}, u32[]{:S(2)}, u32[]{:S(2)}) collective-permute-start(bf16[2,512,256]{2,1,0:T(8,128)(2,1)} %pad_maximum_fusion), channel_id=1, source_target_pairs={{0,4},{4,0},{8,12},{12,8},{16,20},{20,16},{24,28},{28,24},{1,5},{5... | collective-permute-start | bytes 1572872 | tf_op jit(solution)/shard_map/ppermute | solution.py:310
  38.2 44.9 %copy-start.2 = (s32[1,1,2048]{2,1,0:T(1,128)S(1)}, s32[1,1,2048]{2,1,0:T(1,128)}, u32[]{:S(2)}) copy-start(s32[1,1,2048]{2,1,0:T(1,128)} %param.15) | copy-start | bytes 24580
  38.2 22.7 %copy-start.9 = (bf16[64,2048]{1,0:T(8,128)(2,1)S(1)}, bf16[64,2048]{1,0:T(8,128)(2,1)}, u32[]{:S(2)}) copy-start(bf16[64,2048]{1,0:T(8,128)(2,1)} %get-tuple-element.34) | copy-start | bytes 786436
  38.3 24.3 %copy-start.8 = (bf16[64,2048]{1,0:T(8,128)(2,1)S(1)}, bf16[64,2048]{1,0:T(8,128)(2,1)}, u32[]{:S(2)}) copy-start(bf16[64,2048]{1,0:T(8,128)(2,1)} %get-tuple-element.36) | copy-start | bytes 786436
  38.3 24.4 %copy-start.7 = (bf16[64,2048]{1,0:T(8,128)(2,1)S(1)}, bf16[64,2048]{1,0:T(8,128)(2,1)}, u32[]{:S(2)}) copy-start(bf16[64,2048]{1,0:T(8,128)(2,1)} %get-tuple-element.37) | copy-start | bytes 786436
  38.3 4.6 %collective-permute-start.4 = (bf16[2,2048]{1,0:T(2,128)(2,1)S(1)}, bf16[2,2048]{1,0:T(2,128)(2,1)S(1)}, u32[]{:S(2)}, u32[]{:S(2)}) collective-permute-start(bf16[2,2048]{1,0:T(2,128)(2,1)S(1)} %pad_maximum_fusion.1.own_ref), channel_id=1, source_target_pairs={{0,1},{1,2},{2,3},{3,0},{4,5},{5,6},{6,7},{7,4},{8,9},{9,10},{10,1... | collective-permute-start | bytes 24584 | tf_op jit(solution)/shard_map/ppermute | solution.py:299
  42.9 18.0 %collective-permute-start.12 = (bf16[64,2048]{1,0:T(8,128)(2,1)S(1)}, bf16[64,2048]{1,0:T(8,128)(2,1)S(1)}, u32[]{:S(2)}, u32[]{:S(2)}) collective-permute-start(bf16[64,2048]{1,0:T(8,128)(2,1)S(1)} %constant_dynamic-slice_fusion.3), channel_id=1, source_target_pairs={{0,16},{4,20},{8,24},{12,28},{16,0},{20,4},{24,8},{28,12},{1,17},{... | collective-permute-start | bytes 786440 | tf_op jit(solution)/shard_map/ppermute | solution.py:285
  45.3 17.3 %collective-permute-start.9 = (bf16[64,2048]{1,0:T(8,128)(2,1)}, bf16[64,2048]{1,0:T(8,128)(2,1)S(1)}, u32[]{:S(2)}, u32[]{:S(2)}) collective-permute-start(bf16[64,2048]{1,0:T(8,128)(2,1)} %get-tuple-element.32), channel_id=1, source_target_pairs={{0,4},{4,0},{8,12},{12,8},{16,20},{20,16},{24,28},{28,24},{1,5},{5... | collective-permute-start | bytes 786440 | tf_op jit(solution)/shard_map/ppermute | solution.py:285
  45.3 17.4 %collective-permute-start.10 = (bf16[64,2048]{1,0:T(8,128)(2,1)}, bf16[64,2048]{1,0:T(8,128)(2,1)S(1)}, u32[]{:S(2)}, u32[]{:S(2)}) collective-permute-start(bf16[64,2048]{1,0:T(8,128)(2,1)} %get-tuple-element.33), channel_id=1, source_target_pairs={{0,8},{4,12},{8,0},{12,4},{16,24},{20,28},{24,16},{28,20},{1,9},{5... | collective-permute-start | bytes 786440 | tf_op jit(solution)/shard_map/ppermute | solution.py:285
  45.4 21.5 %collective-permute-start.13 = (bf16[64,2048]{1,0:T(8,128)(2,1)}, bf16[64,2048]{1,0:T(8,128)(2,1)S(1)}, u32[]{:S(2)}, u32[]{:S(2)}) collective-permute-start(bf16[64,2048]{1,0:T(8,128)(2,1)} %get-tuple-element.35), channel_id=1, source_target_pairs={{0,20},{4,16},{8,28},{12,24},{16,4},{20,0},{24,12},{28,8},{1,21},{... | collective-permute-start | bytes 786440 | tf_op jit(solution)/shard_map/ppermute | solution.py:285
  58.9 8.6 %collective-permute-start.16 = (bf16[256,512]{1,0:T(8,128)(2,1)S(1)}, bf16[256,512]{1,0:T(8,128)(2,1)S(1)}, u32[]{:S(2)}, u32[]{:S(2)}) collective-permute-start(bf16[256,512]{1,0:T(8,128)(2,1)S(1)} %get-tuple-element.39.wt_ref), channel_id=1, source_target_pairs={{1,0},{2,1},{3,2},{0,3},{5,4},{6,5},{7,6},{4,7},{9,8},{10,9},{11,1... | collective-permute-start | bytes 786440 | tf_op jit(solution)/shard_map/ppermute | solution.py:318
  60.9 22.2 %collective-permute-start.11 = (bf16[64,2048]{1,0:T(8,128)(2,1)S(1)}, bf16[64,2048]{1,0:T(8,128)(2,1)S(1)}, u32[]{:S(2)}, u32[]{:S(2)}) collective-permute-start(bf16[64,2048]{1,0:T(8,128)(2,1)S(1)} %copy-done.9), channel_id=1, source_target_pairs={{0,12},{4,8},{8,4},{12,0},{16,28},{20,24},{24,20},{28,16},{1,13},{... | collective-permute-start | bytes 786440 | tf_op jit(solution)/shard_map/ppermute | solution.py:285
  62.5 20.6 %collective-permute-start.14 = (bf16[64,2048]{1,0:T(8,128)(2,1)S(1)}, bf16[64,2048]{1,0:T(8,128)(2,1)S(1)}, u32[]{:S(2)}, u32[]{:S(2)}) collective-permute-start(bf16[64,2048]{1,0:T(8,128)(2,1)S(1)} %copy-done.8), channel_id=1, source_target_pairs={{0,24},{4,28},{8,16},{12,20},{16,8},{20,12},{24,0},{28,4},{1,25},{... | collective-permute-start | bytes 786440 | tf_op jit(solution)/shard_map/ppermute | solution.py:285
  62.6 20.5 %collective-permute-start.15 = (bf16[64,2048]{1,0:T(8,128)(2,1)S(1)}, bf16[64,2048]{1,0:T(8,128)(2,1)S(1)}, u32[]{:S(2)}, u32[]{:S(2)}) collective-permute-start(bf16[64,2048]{1,0:T(8,128)(2,1)S(1)} %copy-done.7), channel_id=1, source_target_pairs={{0,28},{4,24},{8,20},{12,16},{16,12},{20,8},{24,4},{28,0},{1,29},{... | collective-permute-start | bytes 786440 | tf_op jit(solution)/shard_map/ppermute | solution.py:285
  66.8 29.5 %collective-permute-start.8 = (bf16[256,512]{1,0:T(8,128)(2,1)S(1)}, bf16[256,512]{1,0:T(8,128)(2,1)S(1)}, u32[]{:S(2)}, u32[]{:S(2)}) collective-permute-start(bf16[256,512]{1,0:T(8,128)(2,1)S(1)} %get-tuple-element.30.wt_ref), channel_id=1, source_target_pairs={{1,0},{2,1},{3,2},{0,3},{5,4},{6,5},{7,6},{4,7},{9,8},{10,9},{11,1... | collective-permute-start | bytes 786440 | tf_op jit(solution)/shard_map/ppermute | solution.py:319
  85.1 36.7 %collective-permute-start.17 = (bf16[64,2048]{1,0:T(8,128)(2,1)S(1)}, bf16[64,2048]{1,0:T(8,128)(2,1)S(1)}, u32[]{:S(2)}, u32[]{:S(2)}) collective-permute-start(bf16[64,2048]{1,0:T(8,128)(2,1)S(1)} %get-tuple-element.40), channel_id=1, source_target_pairs={{0,16},{4,20},{8,24},{12,28},{16,0},{20,4},{24,8},{28,12},{1,17},{... | collective-permute-start | bytes 786440 | tf_op jit(solution)/shard_map/ppermute | solution.py:285
  92.5 35.6 %collective-permute-start.18 = (bf16[64,2048]{1,0:T(8,128)(2,1)S(1)}, bf16[64,2048]{1,0:T(8,128)(2,1)S(1)}, u32[]{:S(2)}, u32[]{:S(2)}) collective-permute-start(bf16[64,2048]{1,0:T(8,128)(2,1)S(1)} %get-tuple-element.41), channel_id=1, source_target_pairs={{0,20},{4,16},{8,28},{12,24},{16,4},{20,0},{24,12},{28,8},{1,21},{... | collective-permute-start | bytes 786440 | tf_op jit(solution)/shard_map/ppermute | solution.py:285
  93.2 34.9 %collective-permute-start.19 = (bf16[64,2048]{1,0:T(8,128)(2,1)S(1)}, bf16[64,2048]{1,0:T(8,128)(2,1)S(1)}, u32[]{:S(2)}, u32[]{:S(2)}) collective-permute-start(bf16[64,2048]{1,0:T(8,128)(2,1)S(1)} %get-tuple-element.42), channel_id=1, source_target_pairs={{0,24},{4,28},{8,16},{12,20},{16,8},{20,12},{24,0},{28,4},{1,25},{... | collective-permute-start | bytes 786440 | tf_op jit(solution)/shard_map/ppermute | solution.py:285
  94.7 33.4 %collective-permute-start.20 = (bf16[64,2048]{1,0:T(8,128)(2,1)S(1)}, bf16[64,2048]{1,0:T(8,128)(2,1)S(1)}, u32[]{:S(2)}, u32[]{:S(2)}) collective-permute-start(bf16[64,2048]{1,0:T(8,128)(2,1)S(1)} %get-tuple-element.43), channel_id=1, source_target_pairs={{0,28},{4,24},{8,20},{12,16},{16,12},{20,8},{24,4},{28,0},{1,29},{... | collective-permute-start | bytes 786440 | tf_op jit(solution)/shard_map/ppermute | solution.py:285
  98.4 29.8 %collective-permute-start.21 = (bf16[64,2048]{1,0:T(8,128)(2,1)S(1)}, bf16[64,2048]{1,0:T(8,128)(2,1)S(1)}, u32[]{:S(2)}, u32[]{:S(2)}) collective-permute-start(bf16[64,2048]{1,0:T(8,128)(2,1)S(1)} %get-tuple-element.44), channel_id=1, source_target_pairs={{0,4},{4,0},{8,12},{12,8},{16,20},{20,16},{24,28},{28,24},{1,5},{5... | collective-permute-start | bytes 786440 | tf_op jit(solution)/shard_map/ppermute | solution.py:285
  121.8 11.6 %collective-permute-start.22 = (bf16[64,2048]{1,0:T(8,128)(2,1)S(1)}, bf16[64,2048]{1,0:T(8,128)(2,1)S(1)}, u32[]{:S(2)}, u32[]{:S(2)}) collective-permute-start(bf16[64,2048]{1,0:T(8,128)(2,1)S(1)} %get-tuple-element.45), channel_id=1, source_target_pairs={{0,8},{4,12},{8,0},{12,4},{16,24},{20,28},{24,16},{28,20},{1,9},{5... | collective-permute-start | bytes 786440 | tf_op jit(solution)/shard_map/ppermute | solution.py:285
  128.1 10.8 %collective-permute-start.23 = (bf16[64,2048]{1,0:T(8,128)(2,1)S(1)}, bf16[64,2048]{1,0:T(8,128)(2,1)S(1)}, u32[]{:S(2)}, u32[]{:S(2)}) collective-permute-start(bf16[64,2048]{1,0:T(8,128)(2,1)S(1)} %get-tuple-element.46), channel_id=1, source_target_pairs={{0,12},{4,8},{8,4},{12,0},{16,28},{20,24},{24,20},{28,16},{1,13},{... | collective-permute-start | bytes 786440 | tf_op jit(solution)/shard_map/ppermute | solution.py:285
  133.4 5.5 %copy-start.6 = (bf16[64,16384]{1,0:T(8,128)(2,1)}, bf16[64,16384]{1,0:T(8,128)(2,1)S(1)}, u32[]{:S(2)}) copy-start(bf16[64,16384]{1,0:T(8,128)(2,1)S(1)} %constant_dynamic-update-slice_fusion.1) | copy-start | bytes 6291460
